TPU v7x, 256 devices: a whole 4x4x8 slice. The times are simulated.
256 devices in a mesh: tm: 4 (over x), chan: 64 (over z, y, core).
Axes of the slice: x: 4, y: 4, z: 8, core: 2. Of those that a mesh axis runs over, the one named last changes fastest.
Arguments:
- voltages: bfloat16 [8, 4, 32768, 512], P(None, None, ('tm', 'chan')), may hold values from -6 to 6
- taps: float32 [4, 512], replicated, may hold values from -3 to 3
- busy_mask: int32 [512], replicated, may hold values from 0 to 1, as said below
- drift_low: int32 [512], replicated, may hold values from -16 to 1
Outputs:
- drift_power: float32 [8, 256, 16, 2048], P(None, 'chan', None, 'tm')
Inputs may be any that keep to these rules, and one draw needn't show every extreme that they name: `busy_mask`: exactly 256 entries are 1.
All inputs are finite; a program needn't handle non-finite values.
Results may differ from a plain program's by a relative error of at most 0.008.
Values may be sent and summed in bfloat16 or wider, within the bound.
A program may use at most 128 MiB of HBM per device.

v0:
```python
import math

import jax
import jax.numpy as jnp
from jax import lax
from jax.sharding import PartitionSpec as P

FA = 32
FB = 64
TAPS = 4
NDRIFT = 16
DSPAN = 16
FSTEP = 4
CH_DEV = 1


def passed_along(block, axis, distance):
    devices = range(lax.axis_size(axis))
    route = [(i - distance, i) for i in devices if i - distance in devices]
    return lax.ppermute(block, axis, route)


def in_blocks(value, dim, devices):
    before, after = (value.shape[:dim], value.shape[dim + 1 :])
    return jnp.moveaxis(value.reshape(*before, devices, -1, *after), dim, 0)


def sum_at_owner(value, axis, dim):
    tiles = in_blocks(value, dim, lax.axis_size(axis))
    arrived = lax.all_to_all(tiles, axis, split_axis=0, concat_axis=0, tiled=True)
    return arrived.astype(jnp.float32).sum(axis=0)


def busy_index(busy_mask, busy_count):
    before = jnp.cumsum(busy_mask) - busy_mask
    slot_ids = jnp.arange(busy_count, dtype=jnp.int32)
    is_slot = (busy_mask[:, None] == 1) & (before[:, None] == slot_ids[None, :])
    positions = jnp.arange(busy_mask.shape[0], dtype=jnp.int32)
    return jnp.sum(jnp.where(is_slot, positions[:, None], 0), axis=0)


def real_dft(sample_pos, freq_ids, length):
    phase_index = sample_pos[:, None] * freq_ids[None, :] % length
    angles = phase_index.astype(jnp.float32) * (2.0 * math.pi / length)
    cosines = jnp.cos(angles)
    sine_table = jnp.sin(angles)
    upper = jnp.stack([cosines, -sine_table], axis=1)
    lower = jnp.stack([sine_table, cosines], axis=1)
    return jnp.stack([upper, lower], axis=0).astype(jnp.bfloat16)


def detect_power(spectra):
    items, lanes, chan_rows, samples = spectra.shape
    step_count = samples // (FA * FB)
    shaped = spectra.reshape(items, 2, 2, chan_rows, step_count, FA, FB)
    short_ids = jnp.arange(FA, dtype=jnp.int32)
    long_ids = jnp.arange(FB, dtype=jnp.int32)
    first_pass = jnp.einsum(
        "xopctab,paqf->xoqctfb",
        shaped,
        real_dft(short_ids, short_ids, FA),
        preferred_element_type=jnp.float32,
    )
    twist = short_ids[:, None] * long_ids[None, :] % (FA * FB)
    twist_angles = twist.astype(jnp.float32) * (2.0 * math.pi / (FA * FB))
    twist_cos = jnp.cos(twist_angles)
    twist_sin = jnp.sin(twist_angles)
    real_part = first_pass[:, :, 0]
    imag_part = first_pass[:, :, 1]
    turned = jnp.stack(
        [
            real_part * twist_cos + imag_part * twist_sin,
            imag_part * twist_cos - real_part * twist_sin,
        ],
        axis=2,
    ).astype(jnp.bfloat16)
    second_pass = jnp.einsum(
        "xoqctfb,qbsg->xosctgf",
        turned,
        real_dft(long_ids, long_ids, FB),
        preferred_element_type=jnp.float32,
    )
    powers = jnp.sum(second_pass * second_pass, axis=(1, 2)) / (4.0 * FA * FB)
    return powers.reshape(items, chan_rows, step_count, FA * FB)


def drift_rows(step_rows, first_step, drift_rates, first_bin, bin_width, pad_width):
    padded = jnp.pad(step_rows, ((0, 0), (0, 0), (0, 0), (pad_width, pad_width)))
    chan_rows = step_rows.shape[1]
    rate_count = drift_rates.shape[1]
    running = jnp.zeros((step_rows.shape[0], chan_rows, rate_count, bin_width), jnp.float32)
    for row_index in range(step_rows.shape[2]):
        step_time = first_step + row_index
        per_slot = []
        for slot_pos in range(chan_rows):
            power_row = padded[:, slot_pos, row_index]
            windows = []
            for rate_pos in range(rate_count):
                start = pad_width + first_bin + drift_rates[slot_pos, rate_pos] * step_time
                windows.append(lax.dynamic_slice_in_dim(power_row, start, bin_width, 1))
            per_slot.append(jnp.stack(windows, axis=1))
        running = running + jnp.stack(per_slot, axis=1)
    return running


def slot_rates(slot_part, drift_low):
    one_hot = slot_part[:, None] == jnp.arange(drift_low.shape[0], dtype=jnp.int32)[None, :]
    low_rates = jnp.sum(jnp.where(one_hot, drift_low[None, :], 0), axis=1)
    return low_rates[:, None] + jnp.arange(NDRIFT, dtype=jnp.int32)[None, :]


def shards(voltages, taps, busy_mask, drift_low):
    tm_count = lax.axis_size("tm")
    chan_devices = lax.axis_size("chan")
    count_of_beams, lanes, spec_dev, chan_count = voltages.shape
    busy_count = CH_DEV * tm_count * chan_devices
    step_count = FSTEP * tm_count
    pad_width = DSPAN * (step_count - 1)
    slot_index = busy_index(busy_mask, busy_count)
    coarse_dft = real_dft(jnp.arange(chan_count, dtype=jnp.int32), slot_index, chan_count)
    following = passed_along(voltages[:, :, : TAPS - 1], ("tm", "chan"), -1)
    extended = jnp.concatenate([voltages, following], axis=2)
    filtered = taps[0] * extended[:, :, 0:spec_dev]
    for tap_index in range(1, TAPS):
        filtered = filtered + taps[tap_index] * extended[:, :, tap_index : tap_index + spec_dev]
    filtered = filtered.astype(jnp.bfloat16).reshape(count_of_beams, 2, 2, spec_dev, chan_count)
    coarse = jnp.einsum(
        "bopsn,pnqr->boqrs", filtered, coarse_dft, preferred_element_type=jnp.float32
    )
    coarse = (
        (coarse * chan_count ** (-0.5))
        .astype(jnp.bfloat16)
        .reshape(count_of_beams, 4, busy_count, spec_dev)
    )
    powers = detect_power(lax.all_to_all(coarse, "chan", split_axis=2, concat_axis=3, tiled=True))
    slot_count = CH_DEV * tm_count
    drift_rates = slot_rates(
        lax.dynamic_slice_in_dim(slot_index, lax.axis_index("chan") * slot_count, slot_count),
        drift_low,
    )
    first_step = lax.axis_index("tm") * FSTEP
    partial_value = drift_rows(powers, first_step, drift_rates, 0, FA * FB, pad_width)
    summed = sum_at_owner(partial_value.astype(jnp.bfloat16), "tm", 3)
    result = summed / step_count
    return result


def solution(mesh):
    in_specs = (P(None, None, ("tm", "chan"), None), P(), P(), P())
    out_specs = P(None, "chan", None, "tm")
    return jax.shard_map(shards, mesh=mesh, in_specs=in_specs, out_specs=out_specs, check_vma=False)
```

profile of v0, /device:TPU:24, one launch (start us, length us, event | category | flops | bytes accessed | tf_op | source)
XLA Modules:
  0.0 274.6 jit_solution(3093850198219904586)
XLA Ops:
  0.0 1.0 slice.191
  1.0 2.1 collective-permute-start
  3.1 4.6 %constant_dynamic-update-slice_fusion.1 = bf16[8,4,131,512]{3,2,1,0:T(8,128)(2,1)} fusion(bf16[8,4,128,512]{3,2,1,0:T(8,128)(2,1)} %param.4), kind=kLoop, calls=%fused_computation.47 | loop fusion | bytes 8388608
  8.6 2.5 negate_convert_fusion
  11.1 0.7 constant_dynamic-update-slice_fusion
  11.9 10.8 %add_convert_fusion = bf16[8,4,128,512]{3,2,1,0:T(8,128)(2,1)S(1)} fusion(bf16[8,4,128,512]{3,2,1,0:T(8,128)(2,1)} %param.4, bf16[8,4,131,512]{3,2,1,0:T(8,128)(2,1)} %constant_dynamic-update-slice_fusion, f32[512]{0:T(512)S(1)} %bitcast.671, f32[512]{0:T(512)S(1)} %bitcast.672, f32[512]{0:T(512)S(1)} %bitcast.670, f32[512]{0:T(512)S(1)} %bitcast.669), kind=kLoop, calls=%fused_computation.2 | loop fusion | flops 25165824 | bytes 20979712 | tf_op jit(solution)/shard_map/convert_element_type | solution.py:126
  22.7 2.7 fusion.17
  25.5 3.0 %copy.31 = bf16[8,4,256,128]{3,1,0,2:T(4,128)(2,1)} copy(bf16[8,4,256,128]{3,2,1,0:T(8,128)(2,1)S(1)} %bitcast.410) | data formatting | bytes 4194304 | tf_op jit(solution)/shard_map/reshape | solution.py:133
  28.5 11.8 %all-to-all-start = ((bf16[8,4,256,128]{3,1,0,2:T(4,128)(2,1)}), bf16[8,4,256,128]{3,1,0,2:T(4,128)(2,1)S(1)}, u32[]{:S(2)}, u32[]{:S(2)}) async-start(bf16[8,4,256,128]{3,1,0,2:T(4,128)(2,1)} %copy.31), calls=%async_computation | async-start | bytes 4194304 | tf_op jit(solution)/shard_map/all_to_all | solution.py:135
  40.6 0.7 fusion.64
  58.9 0.7 fusion.63
  107.2 0.7 fusion.61
  155.4 0.7 fusion.62
  207.6 1.3 copy-done
  208.9 2.9 %copy.58 = bf16[8,4,64,4,128]{4,2,3,1,0:T(8,128)(2,1)S(1)} copy(bf16[8,4,64,4,128]{4,1,0,3,2:T(4,128)(2,1)} %bitcast.409) | data formatting | bytes 4194304 | tf_op jit(solution)/shard_map/all_to_all | solution.py:135
  211.8 3.3 %reshape.1398 = bf16[8,2,2,4,4,32,64]{6,5,4,3,2,1,0:T(8,128)(2,1)} reshape(bf16[8,4,4,64,128]{4,3,2,1,0:T(8,128)(2,1)S(1)} %bitcast.408) | data formatting | bytes 4194304 | tf_op jit(solution)/shard_map/reshape | solution.py:55
  215.1 3.5 %fusion.11 = f32[8,2,2,4,4,32,64]{6,5,4,3,1,0,2:T(8,128)S(1)} fusion(bf16[8,2,2,4,4,32,64]{6,5,4,3,2,1,0:T(8,128)(2,1)} %reshape.1398, bf16[1,32,2,32]{1,3,0,2:T(8,128)(2,1)S(1)} %get-tuple-element.284, bf16[1,32,2,32]{1,3,0,2:T(8,128)(2,1)S(1)} %get-tuple-element.283), kind=kOutput, calls=%fused_computation.19 | convolution fusion | flops 134234112 | bytes 6299648 | tf_op jit(solution)/shard_map/xopctab,paqf->xoqctfb/dot_general | solution.py:58
  218.6 1.2 add_convert_fusion.1
  219.8 2.3 fusion
  222.4 2.8 %copy.35 = f32[8,4,4,64,32]{4,3,0,2,1:T(8,128)} copy(f32[8,4,4,64,32]{3,4,2,1,0:T(8,128)S(1)} %multiply_bitcast_fusion) | data formatting | bytes 2097152 | tf_op jit(solution)/shard_map/div | solution.py:83
  225.1 3.9 %div.19 = f32[8,4,4,2048]{3,0,2,1:T(8,128)S(1)} reshape(f32[8,4,4,64,32]{4,3,0,2,1:T(8,128)} %copy.35) | data formatting | bytes 2097152 | tf_op jit(solution)/shard_map/div | solution.py:83
  240.0 1.7 fusion.16
  241.7 30.9 %all_to_all.20 = bf16[4,8,4,16,512]{4,1,3,2,0:T(8,128)(2,1)S(1)} all-to-all(bf16[4,8,4,16,512]{4,1,3,2,0:T(8,128)(2,1)S(1)} %fusion.16), channel_id=1, replica_groups=mesh['tm'=4,'chan'=64] {'tm'}, dimensions={0} | all-to-all | bytes 4194304 | tf_op jit(solution)/shard_map/all_to_all | solution.py:30
  273.0 1.6 copy.37
  (305 shorter events, 11.6 us)
Async XLA Ops:
  1.0 6.7 %copy-start.1 = (s32[512]{0:T(512)S(1)}, s32[512]{0:T(512)}, u32[]{:S(2)}) copy-start(s32[512]{0:T(512)} %param.6) | copy-start | bytes 6148
  1.0 7.3 %copy-start.2 = (f32[4,512]{1,0:T(4,128)S(1)}, f32[4,512]{1,0:T(4,128)}, u32[]{:S(2)}) copy-start(f32[4,512]{1,0:T(4,128)} %param.5) | copy-start | bytes 24580
  1.0 10.1 %collective-permute-start = (bf16[8,4,3,512]{3,2,1,0:T(4,128)(2,1)S(1)}, bf16[8,4,3,512]{3,2,1,0:T(4,128)(2,1)S(1)}, u32[]{:S(2)}, u32[]{:S(2)}) collective-permute-start(bf16[8,4,3,512]{3,2,1,0:T(4,128)(2,1)S(1)} %slice.191), channel_id=1, source_target_pairs={{1,0},{2,1},{3,2},{4,3},{5,4},{6,5},{7,6},{8,7},{9,8},{10,9},{11,1... | collective-permute-start | bytes 294920 | tf_op jit(solution)/shard_map/ppermute | solution.py:20
  25.5 14.9 %copy-start.3 = (s32[512]{0:T(512)S(1)}, s32[512]{0:T(512)}, u32[]{:S(2)}) copy-start(s32[512]{0:T(512)} %param.7) | copy-start | bytes 6148
  28.5 179.1 %all-to-all-start = ((bf16[8,4,256,128]{3,1,0,2:T(4,128)(2,1)}), bf16[8,4,256,128]{3,1,0,2:T(4,128)(2,1)S(1)}, u32[]{:S(2)}, u32[]{:S(2)}) async-start(bf16[8,4,256,128]{3,1,0,2:T(4,128)(2,1)} %copy.31), calls=%async_computation | async-start | bytes 4194304 | tf_op jit(solution)/shard_map/all_to_all | solution.py:135
  207.6 1.3 copy-start
where the time goes:
time: 277 us; the launch traced here: 275 us
  between operations  166 us (60%)
  local copies, waits for them, and re-layouts  37.3 us (13%)
  blocking collectives  30.9 us (11%)
  other arithmetic  18.4 us (7%)
  starting transfers between devices  13.9 us (5%)
  matrix products  8.45 us (3%)
    all_to_all x1, blocking collectives, sum_at_owner(): lax.all_to_all(tiles, axis, split_axis=0, concat_axis=0, tiled=True)  30.9 us
    all_to_all x1, starting transfers between devices, shards(): lax.all_to_all(coarse, 'chan', split_axis=2, concat_axis=3, tiled=True)  11.8 us
    convert_element_type x1, other arithmetic, shards(): filtered.astype(jnp.bfloat16)  10.8 us
    unnamed x249, local copies, waits for them, and re-layouts  7.68 us
    dynamic_slice x16, local copies, waits for them, and re-layouts, drift_rows(): windows.append(lax.dynamic_slice_in_dim(power_row, start, bin_width, 1))  6.74 us
    div x2, local copies, waits for them, and re-layouts, detect_power(): powers = jnp.sum(second_pass * second_pass, axis=(1, 2)) / (4.0 * FA * FB)  6.61 us
  transfers between devices with their start and end apart: 2, of which 0 were waited for; matrix products, arithmetic and copies ran while one was open for 4% of the time, Pallas kernels for 0%

commit v1 on v0

v1 whole, which is shorter than its diff:
```python
import functools
import math

import jax
import jax.numpy as jnp
import numpy as np
from jax import lax
from jax.experimental import pallas as pl
from jax.experimental.pallas import tpu as pltpu
from jax.sharding import PartitionSpec as P

TAPS = 4
NDRIFT = 16
SRC = 16
SEG = 128
FINE = SRC * SEG
HALO = 8
BINS = 512
WIN = BINS // SEG + 2
PAD = 2
BLOCKS = PAD + SRC + 6
STRIDE = 72
VMEM_LIMIT = 60 * 1024 * 1024


def coarse_table(channels):
    n = np.arange(channels, dtype=np.int64)
    angle = ((n[:, None] * n[None, :]) % channels) * (2.0 * math.pi / channels)
    cos, sin = np.cos(angle), np.sin(angle)
    table = np.concatenate([cos, sin, -sin, cos], axis=1)
    return jnp.asarray(table.astype(np.float32)).astype(jnp.bfloat16)


def segment_table():
    s = np.arange(SEG, dtype=np.int64)
    lane = np.arange(SEG, dtype=np.int64)
    g = (lane % 16) * 8 + lane // 16
    angle = ((s[:, None] * g[None, :]) % SEG) * (2.0 * math.pi / SEG)
    cos, sin = np.cos(angle), np.sin(angle)
    table = np.concatenate(
        [np.concatenate([cos, -sin], axis=1), np.concatenate([sin, cos], axis=1)], axis=0
    )
    return jnp.asarray(table.astype(np.float32)).astype(jnp.bfloat16)


def twist_table():
    f = np.arange(SRC, dtype=np.int64)
    s = np.arange(SEG, dtype=np.int64)
    angle = ((f[:, None] * s[None, :]) % FINE) * (2.0 * math.pi / FINE)
    return jnp.asarray(np.stack([np.cos(angle), np.sin(angle)]).astype(np.float32))


def quarter_turns(value, count):
    re, im = value
    count %= 4
    if count == 0:
        return re, im
    if count == 1:
        return im, -re
    if count == 2:
        return -re, -im
    return -im, re


def turned_by(value, cos, sin):
    re, im = value
    return re * cos + im * sin, im * cos - re * sin


def added(left, right):
    return left[0] + right[0], left[1] + right[1]


def dropped(left, right):
    return left[0] - right[0], left[1] - right[1]


def dft4(values):
    a = added(values[0], values[2])
    b = dropped(values[0], values[2])
    c = added(values[1], values[3])
    d = quarter_turns(dropped(values[1], values[3]), 1)
    return [added(a, c), added(b, d), dropped(a, c), dropped(b, d)]


def filter_beam(volt, halo, taps_ref, ext, filt):
    tiles = ext.shape[0]
    for entry in range(4):
        o, p = entry // 2, entry % 2
        rows = volt(entry).astype(jnp.float32)
        tail = halo(entry).astype(jnp.float32)
        for l in range(tiles):
            lanes = slice(l * 128, (l + 1) * 128)
            ext[l, 0:SEG, :] = rows[:, lanes]
            ext[l, SEG : SEG + HALO, :] = tail[:, lanes]
        for l in range(tiles):
            lanes = slice(l * 128, (l + 1) * 128)
            total = taps_ref[0:1, lanes] * ext[l, 0:SEG, :]
            for tap in range(1, TAPS):
                total = total + taps_ref[tap : tap + 1, lanes] * ext[l, tap : tap + SEG, :]
            column = (p * tiles + l) * 128
            filt[o * SEG : (o + 1) * SEG, column : column + 128] = total.astype(jnp.bfloat16)


def coarse_of(filt, dft_ref, q, scale):
    depth = filt.shape[1]
    weights = dft_ref[:, q * depth : (q + 1) * depth]
    out = lax.dot_general(
        weights, filt[...], (((1,), (1,)), ((), ())), preferred_element_type=jnp.float32
    )
    return (out * scale).astype(jnp.bfloat16)


def coarse_kernel(volt_ref, halo_ref, taps_ref, dft_ref, out_ref, ext, filt):
    filter_beam(lambda i: volt_ref[0, i], lambda i: halo_ref[0, i], taps_ref, ext, filt)
    scale = taps_ref.shape[1] ** -0.5
    for q in range(2):
        block = coarse_of(filt, dft_ref, q, scale)
        for d in range(SRC):
            for o in range(2):
                out_ref[d, 0, o, q] = block[d * 16 : (d + 1) * 16, o * SEG : (o + 1) * SEG]


def fine_beam(load, twist_ref, seg_ref, turned, spread, beam):
    for o in range(2):
        inner = []
        for b in range(4):
            group = []
            for a in range(4):
                src = 4 * a + b
                group.append(
                    (load(src, o, 0).astype(jnp.float32), load(src, o, 1).astype(jnp.float32))
                )
            row = dft4(group)
            for f0 in range(1, 4):
                if b:
                    angle = 2.0 * math.pi * b * f0 / 16
                    row[f0] = turned_by(row[f0], math.cos(angle), math.sin(angle))
            inner.append(row)
        for f0 in range(4):
            outs = dft4([inner[b][f0] for b in range(4)])
            for f1 in range(4):
                f = f0 + 4 * f1
                value = outs[f1]
                if f:
                    value = turned_by(value, twist_ref[0, f : f + 1, :], twist_ref[1, f : f + 1, :])
                rows = slice((o * SRC + f) * 16, (o * SRC + f + 1) * 16)
                turned[rows, 0:SEG] = value[0].astype(jnp.bfloat16)
                turned[rows, SEG : 2 * SEG] = value[1].astype(jnp.bfloat16)
    lane = lax.broadcasted_iota(jnp.int32, (8, 128), 1)
    power = None
    for o in range(2):
        second = jnp.dot(
            turned[o * 256 : (o + 1) * 256, :], seg_ref[...], preferred_element_type=jnp.float32
        )
        re, im = second[:, 0:SEG], second[:, SEG : 2 * SEG]
        squares = re * re + im * im
        power = squares if power is None else power + squares
    power = power * (1.0 / (4.0 * FINE))
    for half in range(2):
        blocks = [power[f * 16 + half * 8 : f * 16 + half * 8 + 8, :] for f in range(SRC)]
        for bit in range(4):
            shift = 1 << bit
            upper = (lane & shift) != 0
            for f in range(SRC):
                if f & shift:
                    continue
                low, high = blocks[f], blocks[f | shift]
                blocks[f] = jnp.where(upper, pltpu.roll(high, shift, 1), low)
                blocks[f | shift] = jnp.where(upper, high, pltpu.roll(low, 128 - shift, 1))
        for h in range(SRC):
            spread[PAD + h, pl.ds(half * 64 + beam, 8, stride=8), :] = blocks[h]


def clear_pads(spread):
    zero = jnp.zeros((128, 128), jnp.float32)
    for h in range(PAD):
        spread[h] = zero
    for h in range(PAD + SRC, BLOCKS):
        spread[h] = zero


def shifted_windows(step, low_ref, spread, store):
    lane = lax.broadcasted_iota(jnp.int32, (8, 128), 1)
    count = 4 * 3 + WIN

    def windows(channel):
        start = low_ref[channel] * step + PAD * 128
        first = start // 128
        rest = start - first * 128
        rows = pl.ds(pl.multiple_of(channel * 8, 8), 8)
        rolled = [
            pltpu.roll(spread[first + i, rows, :], lax.rem(128 - rest, 128), 1) for i in range(count + 1)
        ]
        keep = lane < 128 - rest
        return [jnp.where(keep, rolled[i], rolled[i + 1]) for i in range(count)]

    def pair(i, carry):
        left, right = windows(2 * i), windows(2 * i + 1)
        for x in range(4):
            for l in range(WIN):
                value = jnp.concatenate([left[4 * x + l], right[4 * x + l]], axis=0)
                store(x, i // 2, l, lax.rem(i, 2) * 16, value.astype(jnp.bfloat16))
        return carry

    lax.fori_loop(0, 8, pair, 0)


def fine_kernel(step_ref, low_ref, got_ref, twist_ref, seg_ref, out_ref, turned, spread):
    beam = pl.program_id(0)

    @pl.when(beam == 0)
    def _():
        clear_pads(spread)

    fine_beam(lambda src, o, q: got_ref[src, 0, o, q], twist_ref, seg_ref, turned, spread, beam)

    @pl.when(beam == pl.num_programs(0) - 1)
    def _():
        def store(x, m, l, rows, value):
            out_ref[x, m, l, pl.ds(pl.multiple_of(rows, 16), 16), :] = value

        shifted_windows(step_ref[0], low_ref, spread, store)


def drift_kernel(got_ref, out_ref, rows, sums):
    steps = got_ref.shape[0]
    lane = lax.broadcasted_iota(jnp.int32, (8, 128), 1)
    for t in range(steps):
        for l in range(WIN):
            for pair in range(2):
                value = got_ref[t, l, pair * 16 : (pair + 1) * 16, :].astype(jnp.float32)
                rows[2 * pair, t, l] = value[0:8]
                rows[2 * pair + 1, t, l] = value[8:16]

    def channel(ch, carry):
        for j in range(NDRIFT):
            total = [None] * 4
            for t in range(steps):
                first, rest = (j * t) // 128, (j * t) % 128
                if rest == 0:
                    parts = [rows[ch, t, first + l] for l in range(4)]
                else:
                    rolled = [pltpu.roll(rows[ch, t, first + l], 128 - rest, 1) for l in range(5)]
                    parts = [
                        jnp.where(lane < 128 - rest, rolled[l], rolled[l + 1]) for l in range(4)
                    ]
                total = [p if s is None else s + p for s, p in zip(total, parts)]
            for l in range(4):
                sums[l, pl.ds(ch * 16 + j, 8, stride=STRIDE), :] = total[l] * (1.0 / steps)
        return carry

    lax.fori_loop(0, 4, channel, 0)
    for beam in range(8):
        for ch in range(4):
            start = beam * STRIDE + ch * 16
            for l in range(4):
                out_ref[beam, ch, :, l * 128 : (l + 1) * 128] = sums[l, start : start + 16, :]


def owner_z(pair, half, m):
    return 2 * m + half


def device_slots(pair, half, inner):
    m = jnp.arange(4, dtype=jnp.int32)
    owner = owner_z(pair, half, m) * 8 + inner
    return (owner[:, None] * 4 + jnp.arange(4, dtype=jnp.int32)[None, :]).reshape(16)


def shards(voltages, taps, busy_mask, drift_low):
    beams, lanes, seg, channels = voltages.shape
    tm_count = lax.axis_size("tm")
    chan_count = lax.axis_size("chan")
    tm, chan = lax.axis_index("tm"), lax.axis_index("chan")
    pair, pos = chan // SRC, chan % SRC
    step = (tm * (chan_count // SRC) + pair).astype(jnp.int32)

    total = tm_count * chan_count
    route = [(i + 1, i) for i in range(total - 1)]
    halo = lax.ppermute(voltages[:, :, :HALO], ("tm", "chan"), route)

    places = jnp.arange(SRC, dtype=jnp.int32)
    slots = jax.vmap(lambda d: device_slots(pair, d // 8, d % 8))(places).reshape(-1)
    before = jnp.cumsum(busy_mask) - busy_mask
    one_hot = (busy_mask[None, :] == 1) & (before[None, :] == slots[:, None])
    dft = jnp.dot(
        one_hot.astype(jnp.bfloat16), coarse_table(channels), preferred_element_type=jnp.float32
    ).astype(jnp.bfloat16)
    lows = jnp.sum(jnp.where(one_hot, drift_low[None, :], 0), axis=1).reshape(SRC, 16)
    low = jnp.sum(jnp.where(places[:, None] == pos, lows, 0), axis=0)

    sent = pl.pallas_call(
        coarse_kernel,
        grid=(beams,),
        in_specs=[
            pl.BlockSpec((1, 4, seg, channels), lambda b: (b, 0, 0, 0)),
            pl.BlockSpec((1, 4, HALO, channels), lambda b: (b, 0, 0, 0)),
            pl.BlockSpec(taps.shape, lambda b: (0, 0)),
            pl.BlockSpec(dft.shape, lambda b: (0, 0)),
        ],
        out_specs=pl.BlockSpec((SRC, 1, 2, 2, 16, SEG), lambda b: (0, b, 0, 0, 0, 0)),
        out_shape=jax.ShapeDtypeStruct((SRC, beams, 2, 2, 16, SEG), jnp.bfloat16),
        scratch_shapes=[
            pltpu.VMEM((channels // 128, SEG + HALO, 128), jnp.float32),
            pltpu.VMEM((2 * SEG, 2 * channels), jnp.bfloat16),
        ],
        compiler_params=pltpu.CompilerParams(vmem_limit_bytes=VMEM_LIMIT),
    )(voltages, halo, taps, dft)

    groups = [[g * SRC + i for i in range(SRC)] for g in range(chan_count // SRC)]
    got = lax.all_to_all(sent, "chan", 0, 0, axis_index_groups=groups, tiled=True)

    windows = pl.pallas_call(
        fine_kernel,
        grid=(beams,),
        in_specs=[
            pl.BlockSpec(memory_space=pltpu.SMEM),
            pl.BlockSpec(memory_space=pltpu.SMEM),
            pl.BlockSpec((SRC, 1, 2, 2, 16, SEG), lambda b: (0, b, 0, 0, 0, 0)),
            pl.BlockSpec((2, SRC, SEG), lambda b: (0, 0, 0)),
            pl.BlockSpec((2 * SEG, 2 * SEG), lambda b: (0, 0)),
        ],
        out_specs=pl.BlockSpec((4, 4, WIN, 32, 128), lambda b: (0, 0, 0, 0, 0)),
        out_shape=jax.ShapeDtypeStruct((4, 4, WIN, 32, 128), jnp.bfloat16),
        scratch_shapes=[
            pltpu.VMEM((2 * SRC * 16, 2 * SEG), jnp.bfloat16),
            pltpu.VMEM((BLOCKS, 128, 128), jnp.float32),
        ],
        compiler_params=pltpu.CompilerParams(vmem_limit_bytes=VMEM_LIMIT),
    )(step[None], low, got, twist_table(), segment_table())

    over_tm = lax.all_to_all(windows, "tm", 0, 0, tiled=True)
    groups = [[i + g * SRC for g in range(chan_count // SRC)] for i in range(SRC)]
    mine = lax.all_to_all(over_tm, "chan", 1, 1, axis_index_groups=groups, tiled=True)
    steps = mine.reshape(tm_count * (chan_count // SRC), WIN, 32, 128)

    return pl.pallas_call(
        drift_kernel,
        out_shape=jax.ShapeDtypeStruct((beams, 4, NDRIFT, BINS), jnp.float32),
        in_specs=[pl.BlockSpec(memory_space=pltpu.VMEM)],
        out_specs=pl.BlockSpec(memory_space=pltpu.VMEM),
        scratch_shapes=[
            pltpu.VMEM((4, steps.shape[0], WIN, 8, 128), jnp.float32),
            pltpu.VMEM((4, 8 * STRIDE, 128), jnp.float32),
        ],
        compiler_params=pltpu.CompilerParams(vmem_limit_bytes=VMEM_LIMIT),
    )(steps)


def solution(mesh):
    in_specs = (P(None, None, ("tm", "chan"), None), P(), P(), P())
    out_specs = P(None, "chan", None, "tm")
    return jax.shard_map(shards, mesh=mesh, in_specs=in_specs, out_specs=out_specs, check_vma=False)
```

time: 277 us -> 122 us (0.44)
  between operations: 166 us -> 0.06 us
  local copies, waits for them, and re-layouts: 37.3 us -> 4.52 us
  waiting for transfers between devices: 0.01 us -> 27.9 us
  Pallas kernels: 0 us -> 25.7 us
  blocking collectives: 30.9 us -> 47.4 us
  other arithmetic: 18.4 us -> 3.51 us
  matrix products: 8.45 us -> 3.32 us
  starting transfers between devices: 13.9 us -> 8.88 us
    all_to_all x1, waiting for transfers between devices: 0.01 us -> 27.9 us  [shards(): lax.all_to_all(sent, 'chan', 0, 0, axis_index_groups=groups, tiled=True)]
    pallas_call x0 -> x3, Pallas kernels: none -> 25.7 us  [the longest x1 9.48 us: shards(): pl.pallas_call(coarse_kernel, grid=(beams,), in_specs=[pl.BlockSpec((1, 4...]
    all_to_all x1 -> x2, blocking collectives: 30.9 us -> 47.4 us  [the longest x1 25.5 us: shards(): lax.all_to_all(over_tm, 'chan', 1, 1, axis_index_groups=groups, tiled=True)]
    convert_element_type x1 -> x0, other arithmetic: 10.8 us -> none  [shards(): filtered.astype(jnp.bfloat16)]
    div x3 -> x0, local copies, waits for them, and re-layouts: 8.19 us -> none  [the longest x2 6.61 us: detect_power(): powers = jnp.sum(second_pass * second_pass, axis=(1, 2)) / (4.0 * FA * FB)]
    dynamic_slice x17 -> x0, local copies, waits for them, and re-layouts: 6.82 us -> none  [the longest x16 6.74 us: drift_rows(): windows.append(lax.dynamic_slice_in_dim(power_row, start, bin_width, 1))]
    reshape x2 -> x1, local copies, waits for them, and re-layouts: 6.25 us -> 0.08 us  [shards(): jnp.sum(jnp.where(one_hot, drift_low[None, :], 0), axis=1).reshape(SRC, 16)]
    unnamed x249 -> x6, local copies, waits for them, and re-layouts: 7.68 us -> 2.08 us
  transfers between devices with their start and end apart: 2 -> 2, of which waited for: 0 -> 1; matrix products, arithmetic and copies ran while one was open for 4% -> 6% of each run, Pallas kernels for 0% -> 0%
where the time goes in v1:
time: 122 us; the launch traced here: 121 us
  blocking collectives  47.4 us (39%)
  waiting for transfers between devices  27.9 us (23%)
  Pallas kernels  25.7 us (21%)
  starting transfers between devices  8.88 us (7%)
  local copies, waits for them, and re-layouts  4.52 us (4%)
  other arithmetic  3.51 us (3%)
  matrix products  3.32 us (3%)
    all_to_all x1, waiting for transfers between devices, shards(): lax.all_to_all(sent, 'chan', 0, 0, axis_index_groups=groups, tiled=True)  27.9 us
    all_to_all x1, blocking collectives, shards(): lax.all_to_all(over_tm, 'chan', 1, 1, axis_index_groups=groups, tiled=True)  25.5 us
    all_to_all x1, blocking collectives, shards(): over_tm = lax.all_to_all(windows, 'tm', 0, 0, tiled=True)  21.9 us
    pallas_call x1, Pallas kernels, shards(): pl.pallas_call(coarse_kernel, grid=(beams,), in_specs=[pl.BlockSpec((1, 4...  9.48 us
    pallas_call x1, Pallas kernels, shards(): pl.pallas_call(fine_kernel, grid=(beams,), in_specs=[pl.BlockSpec(memory_...  8.88 us
    pallas_call x1, Pallas kernels, shards(): pl.pallas_call(drift_kernel, out_shape=jax.ShapeDtypeStruct((beams, 4, ND...  7.3 us
    all_to_all x1, starting transfers between devices, shards(): lax.all_to_all(sent, 'chan', 0, 0, axis_index_groups=groups, tiled=True)  6.79 us
    dot_general x1, matrix products, shards(): jnp.dot(one_hot.astype(jnp.bfloat16), coarse_table(channels), preferred_e...  3.32 us
  transfers between devices with their start and end apart: 2, of which 1 were waited for; matrix products, arithmetic and copies ran while one was open for 6% of the time, Pallas kernels for 0%

profile of v1, /device:TPU:24, one launch (start us, length us, event | category | flops | bytes accessed | tf_op | source)
XLA Modules:
  0.0 121.3 jit_solution(9225850475968573658)
XLA Ops:
  0.0 1.0 slice.12
  1.0 2.1 %collective-permute-start = (bf16[8,4,8,512]{3,2,1,0:T(8,128)(2,1)S(1)}, bf16[8,4,8,512]{3,2,1,0:T(8,128)(2,1)S(1)}, u32[]{:S(2)}, u32[]{:S(2)}) collective-permute-start(bf16[8,4,8,512]{3,2,1,0:T(8,128)(2,1)S(1)} %slice.12), channel_id=1, source_target_pairs={{1,0},{2,1},{3,2},{4,3},{5,4},{6,5},{7,6},{8,7},{9,8},{10,9},{11,1... | collective-permute-start | bytes 786440 | tf_op jit(solution)/shard_map/ppermute | solution.py:281
  3.1 0.7 broadcast_compare_fusion
  3.8 1.0 reduce-window.9
  4.8 0.1 slice.10
  4.9 0.1 slice_reduce_fusion
  5.0 0.8 bitcast_subtract_fusion
  5.8 0.1 copy.12
  5.9 0.1 iota_add_fusion
  6.0 0.1 add.83
  6.1 3.3 %convolution_convert_fusion.dft_ref = bf16[256,2048]{1,0:T(8,128)(2,1)} fusion(bf16[512,2048]{1,0:T(8,128)(2,1)} %constant.83, s32[512]{0:T(512)S(1)} %bitcast_subtract_fusion, s32[256]{0:T(256)S(1)} %add.83, pred[512]{0:T(512)(128)(4,1)S(1)} %broadcast_compare_fusion), kind=kOutput, calls=%fused_computation | convolution fusion | flops 537657344 | bytes 3149312 | tf_op jit(solution)/shard_map/dot_general | solution.py:287
  9.4 0.7 copy-done.1
  10.2 9.5 %shard_map.73 = bf16[16,8,2,2,16,128]{5,4,3,2,1,0:T(8,128)(2,1)} custom-call(bf16[8,4,128,512]{3,2,1,0:T(8,128)(2,1)} %volt_ref.1, bf16[8,4,8,512]{3,2,1,0:T(8,128)(2,1)} %copy-done.1, f32[4,512]{1,0:T(4,128)} %taps_ref.1, bf16[256,2048]{1,0:T(8,128)(2,1)} %convolution_convert_fusion.dft_ref), custom_call_target="tpu_custom_call" | custom-call | tf_op jit(solution)/shard_map/pallas_call | solution.py:293
  19.6 6.8 %all-to-all-start = ((bf16[16,8,2,2,16,128]{5,4,3,2,1,0:T(8,128)(2,1)}), bf16[16,8,2,2,16,128]{5,4,3,2,1,0:T(8,128)(2,1)S(1)}, u32[]{:S(2)}, u32[]{:S(2)}) async-start(bf16[16,8,2,2,16,128]{5,4,3,2,1,0:T(8,128)(2,1)} %shard_map.73), calls=%async_computation | async-start | bytes 4194304 | tf_op jit(solution)/shard_map/all_to_all | solution.py:312
  26.4 0.3 select_reduce_fusion
  26.7 0.1 reshape.117
  26.8 0.6 select_reduce_fusion.1.low_ref
  27.4 27.9 %all-to-all-done.got_ref = bf16[16,8,2,2,16,128]{5,4,3,2,1,0:T(8,128)(2,1)S(1)} async-done(((bf16[16,8,2,2,16,128]{5,4,3,2,1,0:T(8,128)(2,1)}), bf16[16,8,2,2,16,128]{5,4,3,2,1,0:T(8,128)(2,1)S(1)}, u32[]{:S(2)}, u32[]{:S(2)}) %all-to-all-start) | async-done | bytes 2097184 | tf_op jit(solution)/shard_map/all_to_all | solution.py:312
  55.3 1.3 %copy-done = bf16[16,8,2,2,16,128]{5,4,3,2,1,0:T(8,128)(2,1)} copy-done((bf16[16,8,2,2,16,128]{5,4,3,2,1,0:T(8,128)(2,1)}, bf16[16,8,2,2,16,128]{5,4,3,2,1,0:T(8,128)(2,1)S(1)}, u32[]{:S(2)}) %copy-start) | copy-done | bytes 2097176
  56.7 8.9 %shard_map.74 = bf16[4,4,6,32,128]{4,3,2,1,0:T(8,128)(2,1)} custom-call(s32[1]{0:T(128)} %bitcast.step_ref, s32[16]{0:T(128)} %select_reduce_fusion.1.low_ref, bf16[16,8,2,2,16,128]{5,4,3,2,1,0:T(8,128)(2,1)} %copy-done, f32[2,16,128]{2,1,0:T(8,128)} %constant.80.clone.twist_ref, bf16[256,256]{1,0:T(8,128)(2,1)} %constant.84.seg_ref), custom_call_target="tpu_custom_call" | custom-call | tf_op jit(solution)/shard_map/pallas_call | solution.py:314
  65.6 21.9 %all_to_all.15 = bf16[4,4,6,32,128]{4,3,2,1,0:T(8,128)(2,1)S(1)} all-to-all(bf16[4,4,6,32,128]{4,3,2,1,0:T(8,128)(2,1)} %shard_map.74), channel_id=1, replica_groups=mesh['tm'=4,'chan'=64] {'tm'}, dimensions={0} | all-to-all | bytes 1572864 | tf_op jit(solution)/shard_map/all_to_all | solution.py:333
  87.5 25.5 %all_to_all.16 = bf16[4,4,6,32,128]{4,3,2,0,1:T(8,128)(2,1)S(1)} all-to-all(bf16[4,4,6,32,128]{4,3,2,0,1:T(8,128)(2,1)S(1)} %copy.13), channel_id=1, replica_groups={{0,16,32,48},{1,17,33,49},{2,18,34,50},{3,19,35,51},{4,20,36,52},{5,21,..., dimensions={1} | all-to-all | bytes 1572864 | tf_op jit(solution)/shard_map/all_to_all | solution.py:335
  113.0 0.9 copy.14
  114.0 7.3 %shard_map.75 = f32[8,4,16,512]{3,2,1,0:T(8,128)} custom-call(bf16[16,6,32,128]{3,2,1,0:T(8,128)(2,1)} %bitcast.6), custom_call_target="tpu_custom_call" | custom-call | tf_op jit(solution)/shard_map/pallas_call | solution.py:338
  (11 shorter events, 0.2 us)
Async XLA Ops:
  1.0 8.5 %collective-permute-start = (bf16[8,4,8,512]{3,2,1,0:T(8,128)(2,1)S(1)}, bf16[8,4,8,512]{3,2,1,0:T(8,128)(2,1)S(1)}, u32[]{:S(2)}, u32[]{:S(2)}) collective-permute-start(bf16[8,4,8,512]{3,2,1,0:T(8,128)(2,1)S(1)} %slice.12), channel_id=1, source_target_pairs={{1,0},{2,1},{3,2},{4,3},{5,4},{6,5},{7,6},{8,7},{9,8},{10,9},{11,1... | collective-permute-start | bytes 786440 | tf_op jit(solution)/shard_map/ppermute | solution.py:281
  9.4 0.7 copy-start.1
  19.6 6.8 %copy-start.2 = (s32[512]{0:T(512)S(1)}, s32[512]{0:T(512)}, u32[]{:S(2)}) copy-start(s32[512]{0:T(512)} %param.10) | copy-start | bytes 6148
  19.6 35.7 %all-to-all-start = ((bf16[16,8,2,2,16,128]{5,4,3,2,1,0:T(8,128)(2,1)}), bf16[16,8,2,2,16,128]{5,4,3,2,1,0:T(8,128)(2,1)S(1)}, u32[]{:S(2)}, u32[]{:S(2)}) async-start(bf16[16,8,2,2,16,128]{5,4,3,2,1,0:T(8,128)(2,1)} %shard_map.73), calls=%async_computation | async-start | bytes 4194304 | tf_op jit(solution)/shard_map/all_to_all | solution.py:312
  55.3 1.4 %copy-start = (bf16[16,8,2,2,16,128]{5,4,3,2,1,0:T(8,128)(2,1)}, bf16[16,8,2,2,16,128]{5,4,3,2,1,0:T(8,128)(2,1)S(1)}, u32[]{:S(2)}) copy-start(bf16[16,8,2,2,16,128]{5,4,3,2,1,0:T(8,128)(2,1)S(1)} %all-to-all-done.got_ref) | copy-start | bytes 6291460

commit v2 on v1

--- a/solution.py
+++ b/solution.py
@@ -1,4 +1,3 @@
-import functools
 import math
 
 import jax
@@ -16,6 +15,7 @@
 FINE = SRC * SEG
 HALO = 8
 BINS = 512
+MESH = pl.DeviceIdType.MESH
 WIN = BINS // SEG + 2
 PAD = 2
 BLOCKS = PAD + SRC + 6
@@ -109,16 +109,6 @@
         weights, filt[...], (((1,), (1,)), ((), ())), preferred_element_type=jnp.float32
     )
     return (out * scale).astype(jnp.bfloat16)
-
-
-def coarse_kernel(volt_ref, halo_ref, taps_ref, dft_ref, out_ref, ext, filt):
-    filter_beam(lambda i: volt_ref[0, i], lambda i: halo_ref[0, i], taps_ref, ext, filt)
-    scale = taps_ref.shape[1] ** -0.5
-    for q in range(2):
-        block = coarse_of(filt, dft_ref, q, scale)
-        for d in range(SRC):
-            for o in range(2):
-                out_ref[d, 0, o, q] = block[d * 16 : (d + 1) * 16, o * SEG : (o + 1) * SEG]
 
 
 def fine_beam(load, twist_ref, seg_ref, turned, spread, beam):
@@ -206,32 +196,19 @@
     lax.fori_loop(0, 8, pair, 0)
 
 
-def fine_kernel(step_ref, low_ref, got_ref, twist_ref, seg_ref, out_ref, turned, spread):
-    beam = pl.program_id(0)
-
-    @pl.when(beam == 0)
-    def _():
-        clear_pads(spread)
-
-    fine_beam(lambda src, o, q: got_ref[src, 0, o, q], twist_ref, seg_ref, turned, spread, beam)
-
-    @pl.when(beam == pl.num_programs(0) - 1)
-    def _():
-        def store(x, m, l, rows, value):
-            out_ref[x, m, l, pl.ds(pl.multiple_of(rows, 16), 16), :] = value
-
-        shifted_windows(step_ref[0], low_ref, spread, store)
-
-
-def drift_kernel(got_ref, out_ref, rows, sums):
-    steps = got_ref.shape[0]
+def drift_sums(got, rows, sums, out_ref):
+    steps = got.shape[0]
     lane = lax.broadcasted_iota(jnp.int32, (8, 128), 1)
-    for t in range(steps):
+
+    def widen(t, carry):
         for l in range(WIN):
             for pair in range(2):
-                value = got_ref[t, l, pair * 16 : (pair + 1) * 16, :].astype(jnp.float32)
+                value = got[t, l, pair * 16 : (pair + 1) * 16, :].astype(jnp.float32)
                 rows[2 * pair, t, l] = value[0:8]
                 rows[2 * pair + 1, t, l] = value[8:16]
+        return carry
+
+    lax.fori_loop(0, steps, widen, 0)
 
     def channel(ch, carry):
         for j in range(NDRIFT):
@@ -258,8 +235,179 @@
                 out_ref[beam, ch, :, l * 128 : (l + 1) * 128] = sums[l, start : start + 16, :]
 
 
+def search_kernel(
+    low_ref,
+    volt_ref,
+    halo_ref,
+    taps_ref,
+    dft_ref,
+    twist_ref,
+    seg_ref,
+    out_ref,
+    volt,
+    ext,
+    filt,
+    sent,
+    got,
+    turned,
+    spread,
+    packed,
+    taken,
+    rows,
+    sums,
+    volt_sem,
+    sent_sem,
+    got_sem,
+    packed_sem,
+    taken_sem,
+):
+    beams = volt_ref.shape[0]
+    tm, chan = lax.axis_index("tm"), lax.axis_index("chan")
+    tm_count, pairs = lax.axis_size("tm"), lax.axis_size("chan") // SRC
+    pair, pos = lax.div(chan, SRC), lax.rem(chan, SRC)
+    half, inner = lax.div(pos, 8), lax.rem(pos, 8)
+    step = tm * pairs + pair
+    steps = taken.shape[0]
+
+    def load(b):
+        return pltpu.make_async_copy(volt_ref.at[b], volt.at[b], volt_sem.at[b])
+
+    for b in range(beams):
+        load(b).start()
+
+    barrier = pltpu.get_barrier_semaphore()
+
+    def greet_peer(off, carry):
+        peer = pair * SRC + lax.rem(pos + off, SRC)
+        pl.semaphore_signal(barrier, inc=1, device_id={"tm": tm, "chan": peer}, device_id_type=MESH)
+        return carry
+
+    lax.fori_loop(1, SRC, greet_peer, 0)
+    for dx in range(4):
+        for i in range(4):
+            if dx or i:
+                giver = source_chan(pair, half, inner, i)
+                pl.semaphore_signal(
+                    barrier,
+                    inc=1,
+                    device_id={"tm": lax.rem(tm + dx, 4), "chan": giver},
+                    device_id_type=MESH,
+                )
+    clear_pads(spread)
+
+    def exchange(b, source, place, off):
+        peer = lax.rem(pos + off, SRC)
+        return pltpu.make_async_remote_copy(
+            src_ref=sent.at[source, b],
+            dst_ref=got.at[place, b],
+            send_sem=sent_sem.at[b, off],
+            recv_sem=got_sem.at[b, place],
+            device_id={"tm": tm, "chan": pair * SRC + peer},
+            device_id_type=MESH,
+        )
+
+    scale = taps_ref.shape[1] ** -0.5
+
+    def front(b, carry):
+        load(b).wait()
+        filter_beam(lambda i: volt[b, i], lambda i: halo_ref[b, i], taps_ref, ext, filt)
+        for q in range(2):
+            block = coarse_of(filt, dft_ref, q, scale)
+            for d in range(SRC):
+                for o in range(2):
+                    sent[d, b, o, q] = block[d * 16 : (d + 1) * 16, o * SEG : (o + 1) * SEG]
+        got[pos, b] = sent[pos, b]
+
+        @pl.when(b == 0)
+        def _():
+            pl.semaphore_wait(barrier, 2 * SRC - 2)
+
+        def send(off, carry):
+            exchange(b, lax.rem(pos + off, SRC), pos, off).start()
+            return carry
+
+        lax.fori_loop(1, SRC, send, 0)
+        return carry
+
+    lax.fori_loop(0, beams, front, 0)
+
+    def back(b, carry):
+        def arrive(off, carry):
+            peer = lax.rem(pos + off, SRC)
+            exchange(b, peer, peer, off).wait_recv()
+            return carry
+
+        lax.fori_loop(1, SRC, arrive, 0)
+        fine_beam(lambda src, o, q: got[src, b, o, q], twist_ref, seg_ref, turned, spread, b)
+        return carry
+
+    lax.fori_loop(0, beams, back, 0)
+
+    def store(x, m, l, start, value):
+        packed[x, m, l, pl.ds(pl.multiple_of(start, 16), 16), :] = value
+
+    shifted_windows(step, low_ref, spread, store)
+
+    def hand_over(dx, m):
+        x = lax.rem(tm + dx, 4)
+        return pltpu.make_async_remote_copy(
+            src_ref=packed.at[x, m],
+            dst_ref=taken.at[step],
+            send_sem=packed_sem.at[dx, m],
+            recv_sem=taken_sem.at[step],
+            device_id={"tm": x, "chan": owner_z(pair, half, m) * 8 + inner},
+            device_id_type=MESH,
+        )
+
+    for dx in range(4):
+        for m in range(4):
+            if dx or m:
+                hand_over(dx, m).start()
+    taken[step] = packed[tm, 0]
+
+    def collect(off, carry):
+        place = lax.rem(step + off, steps)
+        pltpu.make_async_remote_copy(
+            src_ref=packed.at[0, 0],
+            dst_ref=taken.at[place],
+            send_sem=packed_sem.at[0, 0],
+            recv_sem=taken_sem.at[place],
+            device_id={"tm": tm, "chan": pair * SRC + lax.rem(pos + 1, SRC)},
+            device_id_type=MESH,
+        ).wait_recv()
+        return carry
+
+    lax.fori_loop(1, steps, collect, 0)
+    drift_sums(taken, rows, sums, out_ref)
+
+    def finish(b, carry):
+        def one(off, carry):
+            exchange(b, lax.rem(pos + off, SRC), pos, off).wait_send()
+            return carry
+
+        return lax.fori_loop(1, SRC, one, carry)
+
+    lax.fori_loop(0, beams, finish, 0)
+    for dx in range(4):
+        for m in range(4):
+            if dx or m:
+                hand_over(dx, m).wait_send()
+
+
 def owner_z(pair, half, m):
-    return 2 * m + half
+    return lax.rem(2 * pair + half + (2 * half - 1) * m + 8, 8)
+
+
+def source_chan(pair, half, inner, i):
+    if i == 0:
+        z = 2 * pair + half
+    elif i == 1:
+        z = 2 * pair + half + 2 - 4 * half + 8
+    elif i == 2:
+        z = 2 * pair + half - 1 + 2 * half + 8
+    else:
+        z = 2 * pair + half - 3 + 6 * half + 8
+    return lax.rem(z, 8) * 8 + inner
 
 
 def device_slots(pair, half, inner):
@@ -274,7 +422,6 @@
     chan_count = lax.axis_size("chan")
     tm, chan = lax.axis_index("tm"), lax.axis_index("chan")
     pair, pos = chan // SRC, chan % SRC
-    step = (tm * (chan_count // SRC) + pair).astype(jnp.int32)
 
     total = tm_count * chan_count
     route = [(i + 1, i) for i in range(total - 1)]
@@ -290,62 +437,43 @@
     lows = jnp.sum(jnp.where(one_hot, drift_low[None, :], 0), axis=1).reshape(SRC, 16)
     low = jnp.sum(jnp.where(places[:, None] == pos, lows, 0), axis=0)
 
-    sent = pl.pallas_call(
-        coarse_kernel,
-        grid=(beams,),
+    steps = tm_count * (chan_count // SRC)
+    vmem = pl.BlockSpec(memory_space=pltpu.VMEM)
+    return pl.pallas_call(
+        search_kernel,
+        out_shape=jax.ShapeDtypeStruct((beams, 4, NDRIFT, BINS), jnp.float32),
         in_specs=[
-            pl.BlockSpec((1, 4, seg, channels), lambda b: (b, 0, 0, 0)),
-            pl.BlockSpec((1, 4, HALO, channels), lambda b: (b, 0, 0, 0)),
-            pl.BlockSpec(taps.shape, lambda b: (0, 0)),
-            pl.BlockSpec(dft.shape, lambda b: (0, 0)),
+            pl.BlockSpec(memory_space=pltpu.SMEM),
+            pl.BlockSpec(memory_space=pl.ANY),
+            vmem,
+            vmem,
+            vmem,
+            vmem,
+            vmem,
         ],
-        out_specs=pl.BlockSpec((SRC, 1, 2, 2, 16, SEG), lambda b: (0, b, 0, 0, 0, 0)),
-        out_shape=jax.ShapeDtypeStruct((SRC, beams, 2, 2, 16, SEG), jnp.bfloat16),
+        out_specs=vmem,
         scratch_shapes=[
+            pltpu.VMEM((beams, 4, seg, channels), jnp.bfloat16),
             pltpu.VMEM((channels // 128, SEG + HALO, 128), jnp.float32),
             pltpu.VMEM((2 * SEG, 2 * channels), jnp.bfloat16),
-        ],
-        compiler_params=pltpu.CompilerParams(vmem_limit_bytes=VMEM_LIMIT),
-    )(voltages, halo, taps, dft)
-
-    groups = [[g * SRC + i for i in range(SRC)] for g in range(chan_count // SRC)]
-    got = lax.all_to_all(sent, "chan", 0, 0, axis_index_groups=groups, tiled=True)
-
-    windows = pl.pallas_call(
-        fine_kernel,
-        grid=(beams,),
-        in_specs=[
-            pl.BlockSpec(memory_space=pltpu.SMEM),
-            pl.BlockSpec(memory_space=pltpu.SMEM),
-            pl.BlockSpec((SRC, 1, 2, 2, 16, SEG), lambda b: (0, b, 0, 0, 0, 0)),
-            pl.BlockSpec((2, SRC, SEG), lambda b: (0, 0, 0)),
-            pl.BlockSpec((2 * SEG, 2 * SEG), lambda b: (0, 0)),
-        ],
-        out_specs=pl.BlockSpec((4, 4, WIN, 32, 128), lambda b: (0, 0, 0, 0, 0)),
-        out_shape=jax.ShapeDtypeStruct((4, 4, WIN, 32, 128), jnp.bfloat16),
-        scratch_shapes=[
+            pltpu.VMEM((SRC, beams, 2, 2, 16, SEG), jnp.bfloat16),
+            pltpu.VMEM((SRC, beams, 2, 2, 16, SEG), jnp.bfloat16),
             pltpu.VMEM((2 * SRC * 16, 2 * SEG), jnp.bfloat16),
             pltpu.VMEM((BLOCKS, 128, 128), jnp.float32),
+            pltpu.VMEM((4, 4, WIN, 32, 128), jnp.bfloat16),
+            pltpu.VMEM((steps, WIN, 32, 128), jnp.bfloat16),
+            pltpu.VMEM((4, steps, WIN, 8, 128), jnp.float32),
+            pltpu.VMEM((4, 8 * STRIDE, 128), jnp.float32),
+            pltpu.SemaphoreType.DMA((beams,)),
+            pltpu.SemaphoreType.DMA((beams, SRC)),
+            pltpu.SemaphoreType.DMA((beams, SRC)),
+            pltpu.SemaphoreType.DMA((4, 4)),
+            pltpu.SemaphoreType.DMA((steps,)),
         ],
-        compiler_params=pltpu.CompilerParams(vmem_limit_bytes=VMEM_LIMIT),
-    )(step[None], low, got, twist_table(), segment_table())
-
-    over_tm = lax.all_to_all(windows, "tm", 0, 0, tiled=True)
-    groups = [[i + g * SRC for g in range(chan_count // SRC)] for i in range(SRC)]
-    mine = lax.all_to_all(over_tm, "chan", 1, 1, axis_index_groups=groups, tiled=True)
-    steps = mine.reshape(tm_count * (chan_count // SRC), WIN, 32, 128)
-
-    return pl.pallas_call(
-        drift_kernel,
-        out_shape=jax.ShapeDtypeStruct((beams, 4, NDRIFT, BINS), jnp.float32),
-        in_specs=[pl.BlockSpec(memory_space=pltpu.VMEM)],
-        out_specs=pl.BlockSpec(memory_space=pltpu.VMEM),
-        scratch_shapes=[
-            pltpu.VMEM((4, steps.shape[0], WIN, 8, 128), jnp.float32),
-            pltpu.VMEM((4, 8 * STRIDE, 128), jnp.float32),
-        ],
-        compiler_params=pltpu.CompilerParams(vmem_limit_bytes=VMEM_LIMIT),
-    )(steps)
+        compiler_params=pltpu.CompilerParams(
+            vmem_limit_bytes=VMEM_LIMIT, collective_id=0, has_side_effects=True
+        ),
+    )(low, voltages, halo, taps, dft, twist_table(), segment_table())
 
 
 def solution(mesh):

time: 122 us -> 82.8 us (0.68)
  the two profiles are of different devices: /device:TPU:24 before, /device:TPU:1 now
where the time goes in v2:
time: 82.8 us; the launch traced here: 82.5 us
  Pallas kernels  65.4 us (79%)
  starting transfers between devices  5.11 us (6%)
  local copies, waits for them, and re-layouts  4.37 us (5%)
  other arithmetic  4.21 us (5%)
  matrix products  3.32 us (4%)
    pallas_call x1, Pallas kernels, shards(): pl.pallas_call(search_kernel, out_shape=jax.ShapeDtypeStruct((beams, 4, N...  65.4 us
    ppermute x1, starting transfers between devices, shards(): halo = lax.ppermute(voltages[:, :, :HALO], ('tm', 'chan'), route)  5.11 us
    dot_general x1, matrix products, shards(): jnp.dot(one_hot.astype(jnp.bfloat16), coarse_table(channels), preferred_e...  3.32 us
    unnamed x3, local copies, waits for them, and re-layouts  3.02 us
  transfers between devices with their start and end apart: 1, of which 0 were waited for; matrix products, arithmetic and copies ran while one was open for 10% of the time, Pallas kernels for 0%

profile of v2, /device:TPU:1, one launch (start us, length us, event | category | flops | bytes accessed | tf_op | source)
XLA Modules:
  0.0 82.5 jit_solution(17157679827933928705)
XLA Ops:
  0.0 1.0 %slice.12 = bf16[8,4,8,512]{3,2,1,0:T(8,128)(2,1)S(1)} slice(bf16[8,4,128,512]{3,2,1,0:T(8,128)(2,1)} %volt_ref.1), slice={[0:8], [0:4], [0:8], [0:512]} | slice | bytes 524288 | tf_op jit(solution)/shard_map/slice | solution.py:428
  1.0 5.1 %collective-permute-start = (bf16[8,4,8,512]{3,2,1,0:T(8,128)(2,1)S(1)}, bf16[8,4,8,512]{3,2,1,0:T(8,128)(2,1)S(1)}, u32[]{:S(2)}, u32[]{:S(2)}) collective-permute-start(bf16[8,4,8,512]{3,2,1,0:T(8,128)(2,1)S(1)} %slice.12), channel_id=1, source_target_pairs={{1,0},{2,1},{3,2},{4,3},{5,4},{6,5},{7,6},{8,7},{9,8},{10,9},{11,1... | collective-permute-start | bytes 786440 | tf_op jit(solution)/shard_map/ppermute | solution.py:428
  6.2 0.7 broadcast_compare_fusion
  6.9 1.0 %reduce-window.9 = s32[4,128]{1,0:T(4,128)S(1)} reduce-window(s32[4,128]{1,0:T(4,128)} %bitcast.4, s32[]{:T(128)} %constant.70.clone.1), window={size=1x128 pad=0_0x127_0}, to_apply=%region_0.1 | reduce-window | flops 65024 | bytes 4100 | tf_op jit(solution)/shard_map/reduce-window
  7.8 0.1 slice.10
  8.0 0.1 slice_reduce_fusion
  8.1 0.8 bitcast_subtract_fusion
  8.8 0.1 fusion.6
  8.9 0.1 iota_add_fusion
  9.0 0.1 add.101
  9.1 0.9 %select_reduce_fusion = s32[256]{0:T(256)S(1)} fusion(s32[512]{0:T(512)} %param.10, s32[512]{0:T(512)S(1)} %bitcast_subtract_fusion, s32[256]{0:T(256)S(1)} %add.101, pred[512]{0:T(512)(128)(4,1)S(1)} %broadcast_compare_fusion), kind=kLoop, calls=%fused_computation.1 | loop fusion | flops 524032 | bytes 6656 | tf_op jit(solution)/shard_map/reduce_sum | solution.py:437
  10.0 0.1 reshape.130
  10.1 0.6 select_reduce_fusion.1.low_ref
  10.8 3.3 %convolution_convert_fusion.dft_ref = bf16[256,2048]{1,0:T(8,128)(2,1)} fusion(bf16[512,2048]{1,0:T(8,128)(2,1)} %constant.84, s32[512]{0:T(512)S(1)} %bitcast_subtract_fusion, s32[256]{0:T(256)S(1)} %add.101, pred[512]{0:T(512)(128)(4,1)S(1)} %broadcast_compare_fusion), kind=kOutput, calls=%fused_computation | convolution fusion | flops 537657344 | bytes 3149312 | tf_op jit(solution)/shard_map/dot_general | solution.py:434
  14.1 0.0 collective-permute-done.halo_ref
  14.1 0.0 copy-start
  14.1 0.7 copy-done
  14.8 65.4 %shard_map.73 = f32[8,4,16,512]{3,2,1,0:T(8,128)} custom-call(s32[16]{0:T(128)} %select_reduce_fusion.1.low_ref, bf16[8,4,128,512]{3,2,1,0:T(8,128)(2,1)} %volt_ref.1, bf16[8,4,8,512]{3,2,1,0:T(8,128)(2,1)} %copy-done, f32[4,512]{1,0:T(4,128)} %taps_ref.1, bf16[256,2048]{1,0:T(8,128)(2,1)} %convolution_convert_fusion.dft_ref, ...), custom_call_target="tpu_custom_call" | custom-call | tf_op jit(solution)/shard_map/pallas_call | solution.py:442
  80.2 2.3 %copy.9 = f32[8,4,16,512]{3,2,1,0:T(8,128)} copy(f32[8,4,16,512]{3,2,1,0:T(8,128)} %shard_map.73) | data formatting | bytes 2097152
  (4 shorter events, 0.1 us)
Async XLA Ops:
  1.0 13.1 %collective-permute-start = (bf16[8,4,8,512]{3,2,1,0:T(8,128)(2,1)S(1)}, bf16[8,4,8,512]{3,2,1,0:T(8,128)(2,1)S(1)}, u32[]{:S(2)}, u32[]{:S(2)}) collective-permute-start(bf16[8,4,8,512]{3,2,1,0:T(8,128)(2,1)S(1)} %slice.12), channel_id=1, source_target_pairs={{1,0},{2,1},{3,2},{4,3},{5,4},{6,5},{7,6},{8,7},{9,8},{10,9},{11,1... | collective-permute-start | bytes 786440 | tf_op jit(solution)/shard_map/ppermute | solution.py:428
  14.1 0.7 copy-start

commit v3 on v2

v3 whole, which is shorter than its diff:
```python
import math

import jax
import jax.numpy as jnp
import numpy as np
from jax import lax
from jax.experimental import pallas as pl
from jax.experimental.pallas import tpu as pltpu
from jax.sharding import PartitionSpec as P

TAPS = 4
NDRIFT = 16
DSPAN = 16
SRC = 16
SEG = 128
FINE = SRC * SEG
HALO = 8
BINS = 512
MESH = pl.DeviceIdType.MESH
WIN = BINS // SEG + 2
PAD = 2
BLOCKS = PAD + SRC + 6
STRIDE = 24
CHUNK = 2
MIX = 8 // CHUNK
SETS = 4 // MIX
TILES = WIN * SETS // 2
SLOT = 8 + CHUNK
VMEM_LIMIT = 60 * 1024 * 1024


def coarse_table(channels):
    n = np.arange(channels, dtype=np.int64)
    angle = ((n[:, None] * n[None, :]) % channels) * (2.0 * math.pi / channels)
    cos, sin = np.cos(angle), np.sin(angle)
    table = np.concatenate([cos, sin], axis=1)
    return jnp.asarray(table.astype(np.float32)).astype(jnp.bfloat16)


def segment_table():
    s = np.arange(SEG, dtype=np.int64)
    lane = np.arange(SEG, dtype=np.int64)
    g = (lane % 16) * 8 + lane // 16
    angle = ((s[:, None] * g[None, :]) % SEG) * (2.0 * math.pi / SEG)
    cos, sin = np.cos(angle), np.sin(angle)
    table = np.concatenate(
        [np.concatenate([cos, -sin], axis=1), np.concatenate([sin, cos], axis=1)], axis=0
    )
    return jnp.asarray(table.astype(np.float32)).astype(jnp.bfloat16)


def twist_table():
    f = np.arange(SRC, dtype=np.int64)
    s = np.arange(SEG, dtype=np.int64)
    angle = ((f[:, None] * s[None, :]) % FINE) * (2.0 * math.pi / FINE)
    return jnp.asarray(np.stack([np.cos(angle), np.sin(angle)]).astype(np.float32))


def quarter_turns(value, count):
    re, im = value
    count %= 4
    if count == 0:
        return re, im
    if count == 1:
        return im, -re
    if count == 2:
        return -re, -im
    return -im, re


def turned_by(value, cos, sin):
    re, im = value
    return re * cos + im * sin, im * cos - re * sin


def added(left, right):
    return left[0] + right[0], left[1] + right[1]


def dropped(left, right):
    return left[0] - right[0], left[1] - right[1]


def dft4(values):
    a = added(values[0], values[2])
    b = dropped(values[0], values[2])
    c = added(values[1], values[3])
    d = quarter_turns(dropped(values[1], values[3]), 1)
    return [added(a, c), added(b, d), dropped(a, c), dropped(b, d)]


def filter_beam(volt, halo, taps_ref, ext, filt):
    tiles = ext.shape[0]
    for entry in range(4):
        o, p = entry // 2, entry % 2
        rows = volt(entry).astype(jnp.float32)
        tail = halo(entry).astype(jnp.float32)
        for l in range(tiles):
            lanes = slice(l * 128, (l + 1) * 128)
            ext[l, 0:SEG, :] = rows[:, lanes]
            ext[l, SEG : SEG + HALO, :] = tail[:, lanes]
        for l in range(tiles):
            lanes = slice(l * 128, (l + 1) * 128)
            total = taps_ref[0:1, lanes] * ext[l, 0:SEG, :]
            for tap in range(1, TAPS):
                total = total + taps_ref[tap : tap + 1, lanes] * ext[l, tap : tap + SEG, :]
            column = (p * tiles + l) * 128
            filt[o * SEG : (o + 1) * SEG, column : column + 128] = total.astype(jnp.bfloat16)


def coarse_of(filt, dft_ref, q, scale):
    depth = filt.shape[1]
    weights = dft_ref[:, q * depth : (q + 1) * depth]
    out = lax.dot_general(
        weights, filt[...], (((1,), (1,)), ((), ())), preferred_element_type=jnp.float32
    )
    return (out * scale).astype(jnp.bfloat16)


def fine_beam(load, twist_ref, seg_ref, turned, spread, beam):
    for o in range(2):
        inner = []
        for b in range(4):
            group = []
            for a in range(4):
                src = 4 * a + b
                group.append(
                    (load(src, o, 0).astype(jnp.float32), load(src, o, 1).astype(jnp.float32))
                )
            row = dft4(group)
            for f0 in range(1, 4):
                if b:
                    angle = 2.0 * math.pi * b * f0 / 16
                    row[f0] = turned_by(row[f0], math.cos(angle), math.sin(angle))
            inner.append(row)
        for f0 in range(4):
            outs = dft4([inner[b][f0] for b in range(4)])
            for f1 in range(4):
                f = f0 + 4 * f1
                value = outs[f1]
                if f:
                    value = turned_by(value, twist_ref[0, f : f + 1, :], twist_ref[1, f : f + 1, :])
                rows = slice((o * SRC + f) * 16, (o * SRC + f + 1) * 16)
                turned[rows, 0:SEG] = value[0].astype(jnp.bfloat16)
                turned[rows, SEG : 2 * SEG] = value[1].astype(jnp.bfloat16)
    lane = lax.broadcasted_iota(jnp.int32, (8, 128), 1)
    power = None
    for o in range(2):
        second = jnp.dot(
            turned[o * 256 : (o + 1) * 256, :], seg_ref[...], preferred_element_type=jnp.float32
        )
        re, im = second[:, 0:SEG], second[:, SEG : 2 * SEG]
        squares = re * re + im * im
        power = squares if power is None else power + squares
    power = power * (1.0 / (4.0 * FINE))
    for half in range(2):
        blocks = [power[f * 16 + half * 8 : f * 16 + half * 8 + 8, :] for f in range(SRC)]
        for bit in range(4):
            shift = 1 << bit
            upper = (lane & shift) != 0
            for f in range(SRC):
                if f & shift:
                    continue
                low, high = blocks[f], blocks[f | shift]
                blocks[f] = jnp.where(upper, pltpu.roll(high, shift, 1), low)
                blocks[f | shift] = jnp.where(upper, high, pltpu.roll(low, 128 - shift, 1))
        for h in range(SRC):
            spread[PAD + h, pl.ds(half * 8 * SLOT + beam, 8, stride=SLOT), :] = blocks[h]


def clear(spread):
    zero = jnp.zeros(spread.shape[1:], jnp.float32)

    def one(h, carry):
        spread[h] = zero
        return carry

    lax.fori_loop(0, BLOCKS, one, 0)


def shifted_windows(step, low_ref, spread, store):
    lane = lax.broadcasted_iota(jnp.int32, (8, 128), 1)
    row = lax.broadcasted_iota(jnp.int32, (8, 128), 0)
    count = 4 * 3 + WIN

    def windows(group, at):
        low = jnp.clip(low_ref[group * MIX + at, 0], -DSPAN, DSPAN)
        start = low * step + PAD * 128
        first = start // 128
        rest = start - first * 128
        base = group * MIX * SLOT + at * 8
        rows = pl.ds(pl.multiple_of(base, 8), 8)
        turn = lax.rem(128 - rest, 128)
        rolled = [pltpu.roll(spread[first + i, rows, :], turn, 1) for i in range(count + 1)]
        keep = lane < 128 - rest
        return [jnp.where(keep, rolled[i], rolled[i + 1]) for i in range(count)]

    def owner(m, carry):
        merged = []
        for part in range(SETS):
            group = m * SETS + part
            value = windows(group, MIX - 1)
            for at in range(MIX - 2, -1, -1):
                below = row < (at + 1) * CHUNK
                value = [jnp.where(below, a, b) for a, b in zip(windows(group, at), value)]
            merged.append(value)
        for x in range(4):
            vectors = [merged[part][4 * x + l] for l in range(WIN) for part in range(SETS)]
            for i in range(TILES):
                value = jnp.concatenate([vectors[2 * i], vectors[2 * i + 1]], axis=0)
                store(x, m, i, value.astype(jnp.bfloat16))
        return carry

    lax.fori_loop(0, 4, owner, 0)


def drift_sums(take, rows, sums, put):
    steps = rows.shape[0]
    lane = lax.broadcasted_iota(jnp.int32, (8, 128), 1)

    def widen(t, carry):
        for i in range(TILES):
            value = take(t, i).astype(jnp.float32)
            for at in range(2):
                l, part = divmod(2 * i + at, SETS)
                rows[t, l, part] = value[at * 8 : (at + 1) * 8]
        return carry

    lax.fori_loop(0, steps, widen, 0)
    for part in range(SETS):
        for j in range(NDRIFT):
            total = [None] * 4
            for t in range(steps):
                first, rest = (j * t) // 128, (j * t) % 128
                if rest == 0:
                    parts = [rows[t, first + l, part] for l in range(4)]
                else:
                    rolled = [pltpu.roll(rows[t, first + l, part], 128 - rest, 1) for l in range(5)]
                    parts = [
                        jnp.where(lane < 128 - rest, rolled[l], rolled[l + 1]) for l in range(4)
                    ]
                total = [p if s is None else s + p for s, p in zip(total, parts)]
            for l in range(4):
                sums[l, pl.ds(j, 8, stride=STRIDE), :] = total[l] * (1.0 / steps)
        for at in range(MIX):
            for b in range(CHUNK):
                start = (at * CHUNK + b) * STRIDE
                for l in range(4):
                    put(part * MIX + at, b, l, sums[l, start : start + NDRIFT, :])


def slot_of(pair, place, index):
    half, inner = place // 8, place % 8
    z = (2 * pair + half + (2 * half - 1) * (index // 4) + 8) % 8
    return (z * 8 + inner) * 4 + index % 4


def choose_channels(pair, pos, mask_ref, low_ref, table, dft, own_low):
    channels = mask_ref.shape[1]
    busy = mask_ref[...] == 1
    ahead = lax.broadcasted_iota(jnp.int32, (channels, channels), 0) < lax.broadcasted_iota(
        jnp.int32, (channels, channels), 1
    )
    before = jnp.dot(
        jnp.broadcast_to(jnp.where(busy, 1.0, 0.0), (8, channels)).astype(jnp.bfloat16),
        jnp.where(ahead, 1.0, 0.0).astype(jnp.bfloat16),
        preferred_element_type=jnp.float32,
    )[0:1].astype(jnp.int32)
    before = jnp.where(busy, before, -1)
    row = lax.broadcasted_iota(jnp.int32, (16 * SRC, 1), 0)
    chosen = before == slot_of(pair, row // 16, row % 16)
    one_hot = jnp.where(chosen, 1.0, 0.0).astype(jnp.bfloat16)
    cos = jnp.dot(one_hot, table[:, 0:channels], preferred_element_type=jnp.float32)
    sin = jnp.dot(one_hot, table[:, channels : 2 * channels], preferred_element_type=jnp.float32)
    dft[:, 0:channels] = cos.astype(jnp.bfloat16)
    dft[:, channels : 2 * channels] = sin.astype(jnp.bfloat16)
    dft[:, 2 * channels : 3 * channels] = (-sin).astype(jnp.bfloat16)
    dft[:, 3 * channels : 4 * channels] = cos.astype(jnp.bfloat16)
    row = lax.broadcasted_iota(jnp.int32, (16, 1), 0)
    mine = before == slot_of(pair, pos, row)
    low = jnp.sum(jnp.where(mine, low_ref[...].astype(jnp.float32), 0.0), axis=1, keepdims=True)
    own_low[...] = jnp.broadcast_to(low, own_low.shape).astype(jnp.int32)


def search_kernel(
    mask_ref,
    low_ref,
    volt_ref,
    taps_ref,
    table_ref,
    twist_ref,
    seg_ref,
    out_ref,
    volt,
    halo,
    table,
    dft,
    own_low,
    low_word,
    ext,
    filt,
    sent,
    got,
    turned,
    spread,
    packed,
    taken,
    rows,
    sums,
    result,
    volt_sem,
    table_sem,
    low_sem,
    out_sem,
    halo_sent,
    halo_got,
    sent_sem,
    got_sem,
    packed_sem,
    taken_sem,
):
    beams = volt_ref.shape[0]
    tm, chan = lax.axis_index("tm"), lax.axis_index("chan")
    tm_count, chan_count = lax.axis_size("tm"), lax.axis_size("chan")
    pairs, total = chan_count // SRC, tm_count * chan_count
    pair, pos = lax.div(chan, SRC), lax.rem(chan, SRC)
    half, inner = lax.div(pos, 8), lax.rem(pos, 8)
    step = tm * pairs + pair
    steps = rows.shape[0]
    pieces = beams // CHUNK

    def device(tm_at, chan_at):
        return {"tm": tm_at, "chan": chan_at}

    def along(distance):
        place = lax.rem(tm * chan_count + chan + distance + total, total)
        return device(lax.div(place, chan_count), lax.rem(place, chan_count))

    def load(b):
        return pltpu.make_async_copy(volt_ref.at[b], volt.at[b], volt_sem.at[b])

    load_table = pltpu.make_async_copy(table_ref, table, table_sem)
    load_table.start()
    for b in range(beams):
        load(b).start()

    barrier = pltpu.get_barrier_semaphore()

    def greet(at):
        pl.semaphore_signal(barrier, inc=1, device_id=at, device_id_type=MESH)

    def greet_peer(off, carry):
        greet(device(tm, pair * SRC + lax.rem(pos + off, SRC)))
        return carry

    greet(along(1))
    lax.fori_loop(1, SRC, greet_peer, 0)
    for dx in range(4):
        for i in range(4):
            if dx or i:
                greet(device(lax.rem(tm + dx, 4), source_chan(pair, half, inner, i)))

    def pass_rows(b):
        return pltpu.make_async_remote_copy(
            src_ref=volt_ref.at[b, :, pl.ds(0, HALO), :],
            dst_ref=halo.at[b],
            send_sem=halo_sent.at[b],
            recv_sem=halo_got.at[b],
            device_id=along(-1),
            device_id_type=MESH,
        )

    pl.semaphore_wait(barrier, 2 * SRC - 1)
    for b in range(beams):
        pass_rows(b).start()
    clear(spread)
    load_table.wait()
    choose_channels(pair, pos, mask_ref, low_ref, table, dft, own_low)
    fetch_low = pltpu.make_async_copy(own_low, low_word, low_sem)

    def exchange(b, source, place, off):
        peer = lax.rem(pos + off, SRC)
        return pltpu.make_async_remote_copy(
            src_ref=sent.at[source, b],
            dst_ref=got.at[place, b],
            send_sem=sent_sem.at[b, off],
            recv_sem=got_sem.at[b, place],
            device_id=device(tm, pair * SRC + peer),
            device_id_type=MESH,
        )

    scale = taps_ref.shape[1] ** -0.5
    ends = tm * chan_count + chan == total - 1

    def front(b, carry):
        load(b).wait()
        pass_rows(b).wait_recv()

        def tail(i):
            value = halo[b, i]
            return jnp.where(ends, jnp.zeros_like(value), value)

        filter_beam(lambda i: volt[b, i], tail, taps_ref, ext, filt)
        for q in range(2):
            block = coarse_of(filt, dft, q, scale)
            for d in range(SRC):
                for o in range(2):
                    sent[d, b, o, q] = block[d * 16 : (d + 1) * 16, o * SEG : (o + 1) * SEG]
        got[pos, b] = sent[pos, b]

        def send(off, carry):
            exchange(b, lax.rem(pos + off, SRC), pos, off).start()
            return carry

        lax.fori_loop(1, SRC, send, 0)
        return carry

    lax.fori_loop(0, beams, front, 0)
    fetch_low.start()
    fetch_low.wait()

    def hand_over(q, dx, m):
        x = lax.rem(tm + dx, 4)
        return pltpu.make_async_remote_copy(
            src_ref=packed.at[q, x, m],
            dst_ref=taken.at[q, step],
            send_sem=packed_sem.at[q, dx, m],
            recv_sem=taken_sem.at[q, step],
            device_id=device(x, owner_z(pair, half, m) * 8 + inner),
            device_id_type=MESH,
        )

    def write(q):
        beams_of = pl.ds(q * CHUNK, CHUNK)
        return pltpu.make_async_copy(result.at[beams_of], out_ref.at[beams_of], out_sem.at[q])

    def transform(q):
        def one(k, carry):
            b = q * CHUNK + k

            def arrive(off, carry):
                peer = lax.rem(pos + off, SRC)
                exchange(b, peer, peer, off).wait_recv()
                return carry

            lax.fori_loop(1, SRC, arrive, 0)
            fine_beam(
                lambda src, o, p: got[src, b, o, p], twist_ref, seg_ref, turned, spread, k
            )
            return carry

        lax.fori_loop(0, CHUNK, one, 0)

        def store(x, m, i, value):
            packed[q, x, m, i] = value

        shifted_windows(step, low_word, spread, store)
        for dx in range(4):
            for m in range(4):
                if dx or m:
                    hand_over(q, dx, m).start()
        taken[q, step] = packed[q, tm, 0]

    def collect(q):
        def one(off, carry):
            place = lax.rem(step + off, steps)
            pltpu.make_async_remote_copy(
                src_ref=packed.at[q, 0, 0],
                dst_ref=taken.at[q, place],
                send_sem=packed_sem.at[q, 0, 0],
                recv_sem=taken_sem.at[q, place],
                device_id=device(tm, pair * SRC + lax.rem(pos + 1, SRC)),
                device_id_type=MESH,
            ).wait_recv()
            return carry

        lax.fori_loop(1, steps, one, 0)

        def put(channel, b, l, value):
            result[q * CHUNK + b, channel, :, l * 128 : (l + 1) * 128] = value

        drift_sums(lambda t, i: taken[q, t, i], rows, sums, put)
        write(q).start()

    def back(q, carry):
        @pl.when(q < pieces)
        def _():
            transform(q)

        @pl.when(q > 0)
        def _():
            collect(q - 1)

        return carry

    lax.fori_loop(0, pieces + 1, back, 0)

    def finish(b, carry):
        def one(off, carry):
            exchange(b, lax.rem(pos + off, SRC), pos, off).wait_send()
            return carry

        pass_rows(b).wait_send()
        return lax.fori_loop(1, SRC, one, carry)

    lax.fori_loop(0, beams, finish, 0)

    def finish_piece(q, carry):
        for dx in range(4):
            for m in range(4):
                if dx or m:
                    hand_over(q, dx, m).wait_send()
        write(q).wait()
        return carry

    lax.fori_loop(0, pieces, finish_piece, 0)


def owner_z(pair, half, m):
    return lax.rem(2 * pair + half + (2 * half - 1) * m + 8, 8)


def source_chan(pair, half, inner, i):
    if i == 0:
        z = 2 * pair + half
    elif i == 1:
        z = 2 * pair + half + 2 - 4 * half + 8
    elif i == 2:
        z = 2 * pair + half - 1 + 2 * half + 8
    else:
        z = 2 * pair + half - 3 + 6 * half + 8
    return lax.rem(z, 8) * 8 + inner


def shards(voltages, taps, busy_mask, drift_low):
    beams, lanes, seg, channels = voltages.shape
    steps = lax.axis_size("tm") * (lax.axis_size("chan") // SRC)
    pieces = beams // CHUNK
    vmem = pl.BlockSpec(memory_space=pltpu.VMEM)
    hbm = pl.BlockSpec(memory_space=pl.ANY)
    dma = pltpu.SemaphoreType.DMA
    return pl.pallas_call(
        search_kernel,
        out_shape=jax.ShapeDtypeStruct((beams, 4, NDRIFT, BINS), jnp.float32),
        in_specs=[vmem, vmem, hbm, vmem, hbm, vmem, vmem],
        out_specs=hbm,
        scratch_shapes=[
            pltpu.VMEM((beams, 4, seg, channels), jnp.bfloat16),
            pltpu.VMEM((beams, 4, HALO, channels), jnp.bfloat16),
            pltpu.VMEM((channels, 2 * channels), jnp.bfloat16),
            pltpu.VMEM((16 * SRC, 4 * channels), jnp.bfloat16),
            pltpu.VMEM((16, 128), jnp.int32),
            pltpu.SMEM((16, 128), jnp.int32),
            pltpu.VMEM((channels // 128, SEG + HALO, 128), jnp.float32),
            pltpu.VMEM((2 * SEG, 2 * channels), jnp.bfloat16),
            pltpu.VMEM((SRC, beams, 2, 2, 16, SEG), jnp.bfloat16),
            pltpu.VMEM((SRC, beams, 2, 2, 16, SEG), jnp.bfloat16),
            pltpu.VMEM((2 * SRC * 16, 2 * SEG), jnp.bfloat16),
            pltpu.VMEM((BLOCKS, 16 * SLOT, 128), jnp.float32),
            pltpu.VMEM((pieces, 4, 4, TILES, 16, 128), jnp.bfloat16),
            pltpu.VMEM((pieces, steps, TILES, 16, 128), jnp.bfloat16),
            pltpu.VMEM((steps, WIN, SETS, 8, 128), jnp.float32),
            pltpu.VMEM((4, 8 * STRIDE, 128), jnp.float32),
            pltpu.VMEM((beams, 4, NDRIFT, BINS), jnp.float32),
            dma((beams,)),
            dma,
            dma,
            dma((pieces,)),
            dma((beams,)),
            dma((beams,)),
            dma((beams, SRC)),
            dma((beams, SRC)),
            dma((pieces, 4, 4)),
            dma((pieces, steps)),
        ],
        compiler_params=pltpu.CompilerParams(
            vmem_limit_bytes=VMEM_LIMIT, collective_id=0, has_side_effects=True
        ),
    )(
        busy_mask[None, :],
        drift_low[None, :],
        voltages,
        taps,
        coarse_table(channels),
        twist_table(),
        segment_table(),
    )


def solution(mesh):
    in_specs = (P(None, None, ("tm", "chan"), None), P(), P(), P())
    out_specs = P(None, "chan", None, "tm")
    return jax.shard_map(shards, mesh=mesh, in_specs=in_specs, out_specs=out_specs, check_vma=False)
```

time: 82.8 us -> 60.6 us (0.73)
  the two profiles are of different devices: /device:TPU:1 before, /device:TPU:24 now
where the time goes in v3:
time: 60.6 us; the launch traced here: 60.4 us
  Pallas kernels  58.1 us (96%)
  local copies, waits for them, and re-layouts  2.31 us (4%)
    pallas_call x1, Pallas kernels, shards(): pl.pallas_call(search_kernel, out_shape=jax.ShapeDtypeStruct((beams, 4, N...  58.1 us
    unnamed x1, local copies, waits for them, and re-layouts  2.31 us

profile of v3, /device:TPU:24, one launch (start us, length us, event | category | flops | bytes accessed | tf_op | source)
XLA Modules:
  0.0 60.4 jit_solution(18043913445330594369)
XLA Ops:
  0.0 58.1 %shard_map.73 = f32[8,4,16,512]{3,2,1,0:T(8,128)} custom-call(s32[1,512]{1,0:T(1,128)} %bitcast.2, s32[1,512]{1,0:T(1,128)} %bitcast.3, bf16[8,4,128,512]{3,2,1,0:T(8,128)(2,1)} %volt_ref.1, f32[4,512]{1,0:T(4,128)} %taps_ref.1, bf16[512,1024]{1,0:T(8,128)(2,1)} %constant.10.table_ref, f32[2,16,128]{2,1,0:T(8,128)} %constant.7.clone.twist_ref, ...), custom_call_target="tpu_custom_call" | custom-call | tf_op jit(solution)/shard_map/pallas_call | solution.py:542
  58.1 2.3 %copy.9 = f32[8,4,16,512]{3,2,1,0:T(8,128)} copy(f32[8,4,16,512]{3,2,1,0:T(8,128)} %shard_map.73) | data formatting | bytes 2097152

commit v4 on v3

v4 whole, which is shorter than its diff:
```python
import math

import jax
import jax.numpy as jnp
import numpy as np
from jax import lax
from jax.experimental import pallas as pl
from jax.experimental.pallas import tpu as pltpu
from jax.sharding import PartitionSpec as P

TAPS = 4
DEPTH = 3
NDRIFT = 16
DSPAN = 16
SRC = 16
SEG = 128
FINE = SRC * SEG
HALO = 8
BINS = 512
MESH = pl.DeviceIdType.MESH
WIN = BINS // SEG + 2
PAD = 2
BLOCKS = PAD + SRC + 6
STRIDE = 24
VECTORS = WIN // 2
SLOT = 10
VMEM_LIMIT = 60 * 1024 * 1024


def coarse_table(channels):
    n = np.arange(channels, dtype=np.int64)
    angle = ((n[:, None] * n[None, :]) % channels) * (2.0 * math.pi / channels)
    cos, sin = np.cos(angle), np.sin(angle)
    table = np.concatenate([cos, sin], axis=1)
    return jnp.asarray(table.astype(np.float32)).astype(jnp.bfloat16)


def segment_table():
    s = np.arange(SEG, dtype=np.int64)
    lane = np.arange(SEG, dtype=np.int64)
    g = (lane % 16) * 8 + lane // 16
    angle = ((s[:, None] * g[None, :]) % SEG) * (2.0 * math.pi / SEG)
    cos, sin = np.cos(angle), np.sin(angle)
    table = np.concatenate(
        [np.concatenate([cos, -sin], axis=1), np.concatenate([sin, cos], axis=1)], axis=0
    )
    return jnp.asarray(table.astype(np.float32)).astype(jnp.bfloat16)


def twist_table():
    f = np.arange(SRC, dtype=np.int64)
    s = np.arange(SEG, dtype=np.int64)
    angle = ((f[:, None] * s[None, :]) % FINE) * (2.0 * math.pi / FINE)
    return jnp.asarray(np.stack([np.cos(angle), np.sin(angle)]).astype(np.float32))


def quarter_turns(value, count):
    re, im = value
    count %= 4
    if count == 0:
        return re, im
    if count == 1:
        return im, -re
    if count == 2:
        return -re, -im
    return -im, re


def turned_by(value, cos, sin):
    re, im = value
    return re * cos + im * sin, im * cos - re * sin


def added(left, right):
    return left[0] + right[0], left[1] + right[1]


def dropped(left, right):
    return left[0] - right[0], left[1] - right[1]


def dft4(values):
    a = added(values[0], values[2])
    b = dropped(values[0], values[2])
    c = added(values[1], values[3])
    d = quarter_turns(dropped(values[1], values[3]), 1)
    return [added(a, c), added(b, d), dropped(a, c), dropped(b, d)]


def filter_beam(volt, taps_ref, ext, filt):
    tiles = ext.shape[0]
    for entry in range(4):
        o, p = entry // 2, entry % 2
        rows = volt(entry).astype(jnp.float32)
        for l in range(tiles):
            ext[l, 0:SEG, :] = rows[:, l * 128 : (l + 1) * 128]
        for l in range(tiles):
            lanes = slice(l * 128, (l + 1) * 128)
            total = taps_ref[0:1, lanes] * ext[l, 0:SEG, :]
            for tap in range(1, TAPS):
                total = total + taps_ref[tap : tap + 1, lanes] * ext[l, tap : tap + SEG, :]
            column = (p * tiles + l) * 128
            filt[o * SEG : (o + 1) * SEG, column : column + 128] = total.astype(jnp.bfloat16)


def lead_rows(head, taps_ref, first):
    channels = taps_ref.shape[1]
    row = lax.broadcasted_iota(jnp.int32, (8, channels), 0)
    keep = row < TAPS - 1

    def beam_rows(b, p):
        both = []
        for o in range(2):
            rows = jnp.where(keep, head[b, 2 * o + p].astype(jnp.float32), 0.0)
            total = rows * taps_ref[TAPS - 1 : TAPS, :]
            for back in range(1, TAPS - 1):
                tap = TAPS - 1 - back
                total = total + pltpu.roll(rows * taps_ref[tap : tap + 1, :], back, 0)
            both.append(jnp.where(keep, total, 0.0))
        return both[0] + pltpu.roll(both[1], 4, 0)

    def one(i, carry):
        for p in range(2):
            value = jnp.concatenate([beam_rows(2 * i, p), beam_rows(2 * i + 1, p)], axis=0)
            value = value.astype(jnp.bfloat16)
            for copy in range(2):
                rows = pl.ds(pl.multiple_of(copy * 64 + i * 16, 16), 16)
                first[rows, p * channels : (p + 1) * channels] = value
        return carry

    lax.fori_loop(0, head.shape[0] // 2, one, 0)


def coarse_of(filt, dft_ref, q, scale):
    depth = filt.shape[1]
    weights = dft_ref[:, q * depth : (q + 1) * depth]
    out = lax.dot_general(
        weights, filt[...], (((1,), (1,)), ((), ())), preferred_element_type=jnp.float32
    )
    return out * scale


def fine_beam(load, twist_ref, seg_ref, turned, spread):
    for o in range(2):
        inner = []
        for b in range(4):
            group = []
            for a in range(4):
                src = 4 * a + b
                group.append(
                    (load(src, o, 0), load(src, o, 1))
                )
            row = dft4(group)
            for f0 in range(1, 4):
                if b:
                    angle = 2.0 * math.pi * b * f0 / 16
                    row[f0] = turned_by(row[f0], math.cos(angle), math.sin(angle))
            inner.append(row)
        for f0 in range(4):
            outs = dft4([inner[b][f0] for b in range(4)])
            for f1 in range(4):
                f = f0 + 4 * f1
                value = outs[f1]
                if f:
                    value = turned_by(value, twist_ref[0, f : f + 1, :], twist_ref[1, f : f + 1, :])
                rows = slice((o * SRC + f) * 16, (o * SRC + f + 1) * 16)
                turned[rows, 0:SEG] = value[0].astype(jnp.bfloat16)
                turned[rows, SEG : 2 * SEG] = value[1].astype(jnp.bfloat16)
    lane = lax.broadcasted_iota(jnp.int32, (8, 128), 1)
    power = None
    for o in range(2):
        second = jnp.dot(
            turned[o * 256 : (o + 1) * 256, :], seg_ref[...], preferred_element_type=jnp.float32
        )
        re, im = second[:, 0:SEG], second[:, SEG : 2 * SEG]
        squares = re * re + im * im
        power = squares if power is None else power + squares
    power = power * (1.0 / (4.0 * FINE))
    for half in range(2):
        blocks = [power[f * 16 + half * 8 : f * 16 + half * 8 + 8, :] for f in range(SRC)]
        for bit in range(4):
            shift = 1 << bit
            upper = (lane & shift) != 0
            for f in range(SRC):
                if f & shift:
                    continue
                low, high = blocks[f], blocks[f | shift]
                blocks[f] = jnp.where(upper, pltpu.roll(high, shift, 1), low)
                blocks[f | shift] = jnp.where(upper, high, pltpu.roll(low, 128 - shift, 1))
        for h in range(SRC):
            for odd in range(2):
                spread[PAD + h, pl.ds(half * 8 * SLOT + odd, 8, stride=SLOT), :] = blocks[h]


def clear(spread):
    zero = jnp.zeros(spread.shape[1:], jnp.float32)

    def one(h, carry):
        spread[h] = zero
        return carry

    lax.fori_loop(0, BLOCKS, one, 0)


def shifted_windows(step, low_ref, spread, store):
    lane = lax.broadcasted_iota(jnp.int32, (8, 128), 1)
    row = lax.broadcasted_iota(jnp.int32, (8, 128), 0)
    count = 4 * 3 + WIN

    def windows(m, at):
        low = jnp.clip(low_ref[m * 4 + at, 0], -DSPAN, DSPAN)
        start = low * step + PAD * 128
        first = start // 128
        rest = start - first * 128
        rows = pl.ds(pl.multiple_of(m * 4 * SLOT + at * 8, 8), 8)
        turn = lax.rem(128 - rest, 128)
        rolled = [pltpu.roll(spread[first + i, rows, :], turn, 1) for i in range(count + 1)]
        keep = lane < 128 - rest
        return [jnp.where(keep, rolled[i], rolled[i + 1]) for i in range(count)]

    def owner(m, carry):
        value = windows(m, 3)
        for at in range(2, -1, -1):
            below = row < (at + 1) * 2
            value = [jnp.where(below, a, b) for a, b in zip(windows(m, at), value)]
        odd = lax.rem(row, 2) == 1
        for x in range(4):
            for k in range(VECTORS):
                block = 4 * x + 2 * k
                store(x, m, k, jnp.where(odd, value[block + 1], value[block]).astype(jnp.bfloat16))
        return carry

    lax.fori_loop(0, 4, owner, 0)


def drift_sums(take, rows, sums, put):
    steps = rows.shape[0]
    lane = lax.broadcasted_iota(jnp.int32, (8, 128), 1)
    odd = lax.rem(lax.broadcasted_iota(jnp.int32, (8, 128), 0), 2) == 1

    def widen(t, carry):
        even = [take(t, k).astype(jnp.float32) for k in range(VECTORS)]
        for k in range(VECTORS):
            rows[t, 2 * k] = even[k]
            if k + 1 < VECTORS:
                rows[t, 2 * k + 1] = jnp.where(
                    odd, pltpu.roll(even[k + 1], 1, 0), pltpu.roll(even[k], 7, 0)
                )
        return carry

    lax.fori_loop(0, steps, widen, 0)
    for j in range(NDRIFT):
        total = [None] * 2
        for t in range(steps):
            first, rest = (j * t) // 128, (j * t) % 128
            parts = []
            for a in range(2):
                value = rows[t, 2 * a + first]
                if rest:
                    following = pltpu.roll(rows[t, 2 * a + first + 1], 128 - rest, 1)
                    value = jnp.where(
                        lane < 128 - rest, pltpu.roll(value, 128 - rest, 1), following
                    )
                parts.append(value)
            total = [p if s is None else s + p for s, p in zip(total, parts)]
        for a in range(2):
            sums[a, pl.ds(j, 8, stride=STRIDE), :] = total[a] * (1.0 / steps)
    for channel in range(4):
        for l in range(4):
            start = (channel * 2 + l % 2) * STRIDE
            put(channel, l, sums[l // 2, start : start + NDRIFT, :])


def slot_of(pair, place, index):
    half, inner = place // 8, place % 8
    z = (2 * pair + half + (2 * half - 1) * (index // 4) + 8) % 8
    return (z * 8 + inner) * 4 + index % 4


def choose_channels(pair, pos, mask_ref, low_ref, table, dft, own_low):
    channels = mask_ref.shape[1]
    busy = mask_ref[...] == 1
    ahead = lax.broadcasted_iota(jnp.int32, (channels, channels), 0) < lax.broadcasted_iota(
        jnp.int32, (channels, channels), 1
    )
    before = jnp.dot(
        jnp.broadcast_to(jnp.where(busy, 1.0, 0.0), (8, channels)).astype(jnp.bfloat16),
        jnp.where(ahead, 1.0, 0.0).astype(jnp.bfloat16),
        preferred_element_type=jnp.float32,
    )[0:1].astype(jnp.int32)
    before = jnp.where(busy, before, -1)
    row = lax.broadcasted_iota(jnp.int32, (16 * SRC, 1), 0)
    chosen = before == slot_of(pair, row // 16, row % 16)
    one_hot = jnp.where(chosen, 1.0, 0.0).astype(jnp.bfloat16)
    cos = jnp.dot(one_hot, table[:, 0:channels], preferred_element_type=jnp.float32)
    sin = jnp.dot(one_hot, table[:, channels : 2 * channels], preferred_element_type=jnp.float32)
    dft[:, 0:channels] = cos.astype(jnp.bfloat16)
    dft[:, channels : 2 * channels] = sin.astype(jnp.bfloat16)
    dft[:, 2 * channels : 3 * channels] = (-sin).astype(jnp.bfloat16)
    dft[:, 3 * channels : 4 * channels] = cos.astype(jnp.bfloat16)
    if own_low is None:
        return
    row = lax.broadcasted_iota(jnp.int32, (16, 1), 0)
    mine = before == slot_of(pair, pos, row)
    low = jnp.sum(jnp.where(mine, low_ref[...].astype(jnp.float32), 0.0), axis=1, keepdims=True)
    own_low[...] = jnp.broadcast_to(low, own_low.shape).astype(jnp.int32)


def search_kernel(
    mask_hbm,
    low_hbm,
    volt_ref,
    taps_hbm,
    table_hbm,
    twist_hbm,
    seg_hbm,
    out_ref,
    mask_ref,
    low_ref,
    taps_ref,
    table,
    twist_ref,
    seg_ref,
    volt,
    head,
    dft,
    lead_dft,
    own_low,
    low_word,
    ext,
    filt,
    sent,
    got,
    first,
    lead,
    leads,
    turned,
    spread,
    packed,
    taken,
    rows,
    sums,
    result,
    volt_sem,
    small_sem,
    low_sem,
    out_sem,
    lead_sent,
    lead_got,
    sent_sem,
    got_sem,
    packed_sem,
    taken_sem,
    ring_sem,
):
    beams = volt_ref.shape[0]
    tm, chan = lax.axis_index("tm"), lax.axis_index("chan")
    tm_count, chan_count = lax.axis_size("tm"), lax.axis_size("chan")
    pairs = chan_count // SRC
    pair, pos = lax.div(chan, SRC), lax.rem(chan, SRC)
    half, inner = lax.div(pos, 8), lax.rem(pos, 8)
    step = tm * pairs + pair
    steps = rows.shape[0]

    def device(tm_at, chan_at):
        return {"tm": tm_at, "chan": chan_at}

    def in_group(distance, place):
        group = lax.rem(step + distance + steps, steps)
        return device(lax.div(group, pairs), lax.rem(group, pairs) * SRC + place)

    def along_z(distance):
        z = lax.rem(2 * pair + half + distance + 8, 8)
        return device(tm, z * 8 + inner)

    def call(far):
        for side in range(2):
            pl.semaphore_signal(
                ring_sem.at[2 * far + side],
                inc=1,
                device_id=along_z((1 - 2 * side) * (far + 1)),
                device_id_type=MESH,
            )

    def hear(far):
        for side in range(2):
            pl.semaphore_wait(ring_sem.at[2 * far + side], 1)

    def load(b):
        return pltpu.make_async_copy(volt_ref.at[b], volt.at[b], volt_sem.at[b])

    small = [
        pltpu.make_async_copy(source, target, small_sem.at[i])
        for i, (source, target) in enumerate(
            [
                (mask_hbm, mask_ref),
                (low_hbm, low_ref),
                (table_hbm, table),
                (taps_hbm, taps_ref),
                (seg_hbm, seg_ref),
                (volt_ref.at[:, :, pl.ds(0, HALO), :], head),
                (twist_hbm, twist_ref),
            ]
        )
    ]
    for copy in small:
        copy.start()
    for b in range(beams):
        load(b).start()

    barrier = pltpu.get_barrier_semaphore()

    def greet(at):
        pl.semaphore_signal(barrier, inc=1, device_id=at, device_id_type=MESH)

    def greet_peer(off, carry):
        greet(device(tm, pair * SRC + lax.rem(pos + off, SRC)))
        return carry

    greet(in_group(1, 0))
    lax.fori_loop(1, SRC, greet_peer, 0)
    for dx in range(1, 4):
        greet(device(lax.rem(tm + dx, 4), chan))
    greet(along_z(2 * half - 1))

    heads = 1 - lax.div(pos + SRC - 1, SRC)
    clear(spread)
    for l in range(ext.shape[0]):
        ext[l, SEG : SEG + HALO, :] = jnp.zeros((HALO, 128), jnp.float32)
    for copy in small[0:3]:
        copy.wait()
    choose_channels(pair, pos, mask_ref, low_ref, table, dft, own_low)
    for copy in small[3:]:
        copy.wait()
    fetch_low = pltpu.make_async_copy(own_low, low_word, low_sem)
    fetch_low.start()
    pl.semaphore_wait(barrier, SRC - 1 + 3 + 1 + SRC * heads)
    call(0)

    def pass_lead(off, place, kind=1):
        return pltpu.make_async_remote_copy(
            src_ref=lead.at[lax.rem(pos + off, SRC)],
            dst_ref=leads.at[place],
            send_sem=lead_sent.at[kind],
            recv_sem=lead_got.at[kind],
            device_id=in_group(-heads, lax.rem(pos + off, SRC)),
            device_id_type=MESH,
        )

    before = lax.rem(pos + SRC - 1, SRC)

    def exchange(b, source, place, off):
        peer = lax.rem(pos + off, SRC)
        return pltpu.make_async_remote_copy(
            src_ref=sent.at[source, b],
            dst_ref=got.at[place, b],
            send_sem=sent_sem.at[b],
            recv_sem=got_sem.at[b],
            device_id=device(tm, pair * SRC + peer),
            device_id_type=MESH,
        )

    others = pl.ds(0, SRC - 1)
    peer_device = device(tm, pair * SRC + lax.rem(pos + 1, SRC))

    def exchange_all(b):
        return pltpu.make_async_remote_copy(
            src_ref=sent.at[others, b],
            dst_ref=got.at[others, b],
            send_sem=sent_sem.at[b],
            recv_sem=got_sem.at[b],
            device_id=peer_device,
            device_id_type=MESH,
        )

    def lead_all():
        return pltpu.make_async_remote_copy(
            src_ref=lead.at[others],
            dst_ref=leads.at[others],
            send_sem=lead_sent.at[1],
            recv_sem=lead_got.at[1],
            device_id=peer_device,
            device_id_type=MESH,
        )

    def hand_over_all(q):
        return pltpu.make_async_remote_copy(
            src_ref=taken.at[q, others],
            dst_ref=taken.at[q, others],
            send_sem=packed_sem.at[q],
            recv_sem=taken_sem.at[q],
            device_id=peer_device,
            device_id_type=MESH,
        )

    scale = taps_ref.shape[1] ** -0.5
    def leading():
        choose_channels(pair - heads, pos, mask_ref, low_ref, table, lead_dft, None)
        lead_rows(head, taps_ref, first)
        blocks = [coarse_of(first, lead_dft, q, scale) for q in range(2)]
        low_lanes = lax.broadcasted_iota(jnp.int32, blocks[0].shape, 1) < 64
        both = jnp.where(low_lanes, blocks[0], blocks[1])
        for d in range(SRC):
            lead[d] = both[d * 16 : (d + 1) * 16, :].astype(jnp.bfloat16)

        def send_lead(off, carry):
            pass_lead(off, before).start()
            return carry

        lax.fori_loop(1, SRC, send_lead, 0)

        @pl.when(heads == 1)
        def _():
            pass_lead(0, before, 0).start()

        @pl.when(heads == 0)
        def _():
            leads[before] = lead[pos]

    def front(b, carry):
        load(b).wait()
        filter_beam(lambda i: volt[b, i], taps_ref, ext, filt)
        for q in range(2):
            block = coarse_of(filt, dft, q, scale)
            for d in range(SRC):
                for o in range(2):
                    value = block[d * 16 : (d + 1) * 16, o * SEG : (o + 1) * SEG]
                    sent[d, b, o, q] = value.astype(jnp.bfloat16)
        got[pos, b] = sent[pos, b]

        def send(off, carry):
            exchange(b, lax.rem(pos + off, SRC), pos, off).start()
            return carry

        lax.fori_loop(1, SRC, send, 0)
        pl.when(b == 0)(leading)
        return carry

    lax.fori_loop(0, beams, front, 0)
    hear(0)
    call(1)
    fetch_low.wait()
    lane = lax.broadcasted_iota(jnp.int32, (16, SEG), 1)

    def arrived(b, src, o, p):
        value = got[src, b, o, p].astype(jnp.float32)
        extra = leads[src].astype(jnp.float32)
        turn = lax.rem(2 * SEG - (TAPS - 1) - p * 64 - (2 * b + o) * 4, SEG)
        start = SEG - (TAPS - 1)
        if src == SRC - 1:
            start = start + (TAPS - 1) * lax.div(step + 1, steps)
        return value + jnp.where(lane >= start, pltpu.roll(extra, turn, 1), 0.0)


    def hand_over(q, dx, m):
        x = lax.rem(tm + dx, 4)
        return pltpu.make_async_remote_copy(
            src_ref=packed.at[q, x, m],
            dst_ref=taken.at[q, step],
            send_sem=packed_sem.at[q],
            recv_sem=taken_sem.at[q],
            device_id=device(x, owner_z(pair, half, m) * 8 + inner),
            device_id_type=MESH,
        )

    def write(q):
        return pltpu.make_async_copy(result.at[q], out_ref.at[q], out_sem.at[q])

    def transform(q):
        exchange_all(q).wait_recv()
        fine_beam(lambda src, o, p: arrived(q, src, o, p), twist_ref, seg_ref, turned, spread)

        def store(x, m, k, value):
            packed[q, x, m, k] = value

        shifted_windows(step, low_word, spread, store)
        for m in range(3, -1, -1):
            for dx in (2, 1, 3, 0):
                if dx or m:
                    hand_over(q, dx, m).start()
        taken[q, step] = packed[q, tm, 0]

    def collect(q):
        hand_over_all(q).wait_recv()

        def put(channel, l, value):
            result[q, channel, :, l * 128 : (l + 1) * 128] = value

        drift_sums(lambda t, k: taken[q, t, k], rows, sums, put)
        write(q).start()

    lead_all().wait_recv()
    hear(1)

    @pl.when(heads == 1)
    def _():
        pass_lead(0, before, 0).wait_recv()

    def finish():
        def one(b, carry):
            exchange_all(b).wait_send()
            return carry

        lax.fori_loop(0, beams, one, 0)
        lead_all().wait_send()

        @pl.when(heads == 1)
        def _():
            pass_lead(0, before, 0).wait_send()

    def back(q, carry):
        @pl.when(q < beams)
        def _():
            transform(q)

        pl.when(q == beams)(finish)

        @pl.when(q >= DEPTH)
        def _():
            collect(q - DEPTH)

        return carry

    lax.fori_loop(0, beams + DEPTH, back, 0)

    def close(q, carry):
        hand_over_all(q).wait_send()
        write(q).wait()
        return carry

    lax.fori_loop(0, beams, close, 0)


def owner_z(pair, half, m):
    return lax.rem(2 * pair + half + (2 * half - 1) * m + 8, 8)


def shards(voltages, taps, busy_mask, drift_low):
    beams, lanes, seg, channels = voltages.shape
    steps = lax.axis_size("tm") * (lax.axis_size("chan") // SRC)
    hbm = pl.BlockSpec(memory_space=pl.ANY)
    dma = pltpu.SemaphoreType.DMA
    return pl.pallas_call(
        search_kernel,
        out_shape=jax.ShapeDtypeStruct((beams, 4, NDRIFT, BINS), jnp.float32),
        in_specs=[hbm] * 7,
        out_specs=hbm,
        scratch_shapes=[
            pltpu.VMEM((1, channels), jnp.int32),
            pltpu.VMEM((1, channels), jnp.int32),
            pltpu.VMEM(taps.shape, jnp.float32),
            pltpu.VMEM((channels, 2 * channels), jnp.bfloat16),
            pltpu.VMEM((2, SRC, SEG), jnp.float32),
            pltpu.VMEM((2 * SEG, 2 * SEG), jnp.bfloat16),
            pltpu.VMEM((beams, 4, seg, channels), jnp.bfloat16),
            pltpu.VMEM((beams, 4, HALO, channels), jnp.bfloat16),
            pltpu.VMEM((16 * SRC, 4 * channels), jnp.bfloat16),
            pltpu.VMEM((16 * SRC, 4 * channels), jnp.bfloat16),
            pltpu.VMEM((16, 128), jnp.int32),
            pltpu.SMEM((16, 128), jnp.int32),
            pltpu.VMEM((channels // 128, SEG + HALO, 128), jnp.float32),
            pltpu.VMEM((2 * SEG, 2 * channels), jnp.bfloat16),
            pltpu.VMEM((SRC, beams, 2, 2, 16, SEG), jnp.bfloat16),
            pltpu.VMEM((SRC, beams, 2, 2, 16, SEG), jnp.bfloat16),
            pltpu.VMEM((beams * 16, 2 * channels), jnp.bfloat16),
            pltpu.VMEM((SRC, 16, SEG), jnp.bfloat16),
            pltpu.VMEM((SRC, 16, SEG), jnp.bfloat16),
            pltpu.VMEM((2 * SRC * 16, 2 * SEG), jnp.bfloat16),
            pltpu.VMEM((BLOCKS, 16 * SLOT, 128), jnp.float32),
            pltpu.VMEM((beams, 4, 4, VECTORS, 8, 128), jnp.bfloat16),
            pltpu.VMEM((beams, steps, VECTORS, 8, 128), jnp.bfloat16),
            pltpu.VMEM((steps, WIN - 1, 8, 128), jnp.float32),
            pltpu.VMEM((2, 8 * STRIDE, 128), jnp.float32),
            pltpu.VMEM((beams, 4, NDRIFT, BINS), jnp.float32),
            dma((beams,)),
            dma((7,)),
            dma,
            dma((beams,)),
            dma((2,)),
            dma((2,)),
            dma((beams,)),
            dma((beams,)),
            dma((beams,)),
            dma((beams,)),
            pltpu.SemaphoreType.REGULAR((4,)),
        ],
        compiler_params=pltpu.CompilerParams(
            vmem_limit_bytes=VMEM_LIMIT, collective_id=0, has_side_effects=True
        ),
    )(
        busy_mask[None, :],
        drift_low[None, :],
        voltages,
        taps,
        coarse_table(channels),
        twist_table(),
        segment_table(),
    )


def solution(mesh):
    in_specs = (P(None, None, ("tm", "chan"), None), P(), P(), P())
    out_specs = P(None, "chan", None, "tm")
    return jax.shard_map(shards, mesh=mesh, in_specs=in_specs, out_specs=out_specs, check_vma=False)
```

time: 60.6 us -> 53.9 us (0.89)
  Pallas kernels: 58.1 us -> 51.5 us
    pallas_call x1, Pallas kernels: 58.1 us -> 51.5 us  [shards(): pl.pallas_call(search_kernel, out_shape=jax.ShapeDtypeStruct((beams, 4, N...]
where the time goes in v4:
time: 53.9 us; the launch traced here: 53.8 us
  Pallas kernels  51.5 us (96%)
  local copies, waits for them, and re-layouts  2.31 us (4%)
    pallas_call x1, Pallas kernels, shards(): pl.pallas_call(search_kernel, out_shape=jax.ShapeDtypeStruct((beams, 4, N...  51.5 us
    unnamed x1, local copies, waits for them, and re-layouts  2.31 us

profile of v4, /device:TPU:24, one launch (start us, length us, event | category | flops | bytes accessed | tf_op | source)
XLA Modules:
  0.0 53.8 jit_solution(16778394549960979318)
XLA Ops:
  0.0 51.5 %shard_map.73 = f32[8,4,16,512]{3,2,1,0:T(8,128)} custom-call(s32[1,512]{1,0:T(1,128)} %bitcast.2, s32[1,512]{1,0:T(1,128)} %bitcast.3, bf16[8,4,128,512]{3,2,1,0:T(8,128)(2,1)} %volt_ref.1, f32[4,512]{1,0:T(4,128)} %taps_hbm.1, bf16[512,1024]{1,0:T(8,128)(2,1)} %constant.10.table_hbm, f32[2,16,128]{2,1,0:T(8,128)} %constant.7.clone.twist_hbm, ...), custom_call_target="tpu_custom_call" | custom-call | tf_op jit(solution)/shard_map/pallas_call | solution.py:643
  51.5 2.3 %copy.9 = f32[8,4,16,512]{3,2,1,0:T(8,128)} copy(f32[8,4,16,512]{3,2,1,0:T(8,128)} %shard_map.73) | data formatting | bytes 2097152
